TPU v7x, 128 devices: a whole 4x4x4 slice. The times are simulated.
128 devices in a mesh: expert: 64 (over y, x, z), etp: 2 (over core).
Axes of the slice: x: 4, y: 4, z: 4, core: 2. Of those that a mesh axis runs over, the one named last changes fastest.
Arguments:
- grad_out: bfloat16 [8192, 3584], P('expert', 'etp'), may hold values from -6 to 6
- combine: bfloat16 [8192, 8], P('expert'), may hold values from 0.099609375 to 2.5
- expert_ids: int32 [8192, 8], P('expert'), may hold values from 0 to 127, all different within a row; in each aligned block of 128 rows (0 to 127, 128 to 255, ...) at most 16 rows name the same one
- saved_gate: bfloat16 [1024, 128, 1024], P(None, 'expert', 'etp'), may hold values from -6 to 6
- saved_up: bfloat16 [1024, 128, 1024], P(None, 'expert', 'etp'), may hold values from -1.5 to 1.5
- gate_weight: bfloat16 [128, 3584, 1024], P('expert', None, 'etp'), may hold values from -0.09375 to 0.09375
- up_weight: bfloat16 [128, 3584, 1024], P('expert', None, 'etp'), may hold values from -0.09375 to 0.09375
- down_weight: bfloat16 [128, 1024, 3584], P('expert', 'etp'), may hold values from -0.09375 to 0.09375
Outputs:
- grad_tokens: bfloat16 [8192, 3584], P('expert', 'etp')
- grad_combine: bfloat16 [8192, 8], P('expert')
Inputs may be any that keep to these rules, and one draw needn't show every extreme that they name: `expert_ids`: each token names 8 different experts. Among the 128 tokens of one block (one index of expert), at most 16 name any one expert, and some blocks reach that bound.
All inputs are finite; a program needn't handle non-finite values.
Results may differ from a plain program's by a relative error of at most 0.012.
Values may be sent and summed in bfloat16 or wider, within the bound.
No kernel may reach another device: no remote copies, remote signals or barrier semaphores. Data moves between devices by JAX's collectives and lax.ppermute only.
A program may use at most 192 MiB of HBM per device.

v0:
```python
import jax
import jax.numpy as jnp
from jax import lax
from jax.sharding import PartitionSpec as P


def copy_for_each(x, axis):
    copies = jnp.broadcast_to(x, (lax.axis_size(axis), *x.shape))
    return lax.all_to_all(copies, axis, split_axis=0, concat_axis=0, tiled=True)


def of_everyone(x, axis):
    return copy_for_each(x, axis).astype(jnp.float32).sum(axis=0)


def slot_layout(expert_ids, groups, per_group, capacity):
    token_count, top_count = expert_ids.shape
    experts = groups * per_group
    matches = expert_ids[:, :, None] == jnp.arange(experts, dtype=jnp.int32)[None, None, :]
    expert_loads = jnp.sum(matches.astype(jnp.int32), axis=1)
    earlier = jnp.cumsum(expert_loads, axis=0) - expert_loads
    position = jnp.sum(jnp.where(matches, earlier[:, None, :], 0), axis=2)
    target = expert_ids // per_group
    local_slot = expert_ids % per_group
    flat_slot = (target * capacity + position) * per_group + local_slot
    slot_total = groups * capacity * per_group
    slot_owner = jnp.full((slot_total,), token_count * top_count, jnp.int32)
    slot_owner = slot_owner.at[flat_slot.reshape(-1)].set(
        jnp.arange(token_count * top_count, dtype=jnp.int32)
    )
    return (flat_slot, slot_owner)


def on_device(
    grad_out, combine, expert_ids, saved_gate, saved_up, gate_weight, up_weight, down_weight
):
    groups = lax.axis_size("expert")
    per_group = gate_weight.shape[0]
    half_width = grad_out.shape[1]
    token_count, top_count = expert_ids.shape
    capacity = saved_gate.shape[0] // groups
    slot_rows_count = groups * capacity
    flat_slot, slot_owner = slot_layout(expert_ids, groups, per_group, capacity)
    source_token = slot_owner // top_count
    weight_flat = jnp.concatenate([combine.reshape(-1), jnp.zeros((1,), jnp.bfloat16)])
    slot_weight = jnp.take(weight_flat, slot_owner, axis=0).reshape(groups, capacity, per_group)
    padded = jnp.concatenate([grad_out, jnp.zeros((1, half_width), jnp.bfloat16)], axis=0)
    outgoing = jnp.take(padded, source_token, axis=0).reshape(
        groups, capacity, per_group, half_width
    )
    arrived, arrived_weight = (
        lax.all_to_all(outgoing, "expert", split_axis=0, concat_axis=0, tiled=True),
        lax.all_to_all(slot_weight, "expert", split_axis=0, concat_axis=0, tiled=True),
    )
    slot_rows = lax.all_gather(
        arrived.reshape(slot_rows_count, per_group, half_width), "etp", axis=2, tiled=True
    )
    grad_hidden = jnp.einsum(
        "rld,lfd->rlf", slot_rows, down_weight, preferred_element_type=jnp.float32
    )
    gate_value = saved_gate.astype(jnp.float32)
    up_value = saved_up.astype(jnp.float32)
    gate_sigmoid = jax.nn.sigmoid(gate_value)
    activated = gate_value * gate_sigmoid
    weight_part = jnp.sum(grad_hidden * activated * up_value, axis=2)
    scaled = arrived_weight.reshape(slot_rows_count, per_group, 1).astype(jnp.float32) * grad_hidden
    grad_gate = (
        scaled * up_value * gate_sigmoid * (1.0 + gate_value * (1.0 - gate_sigmoid))
    ).astype(jnp.bfloat16)
    grad_up = (scaled * activated).astype(jnp.bfloat16)
    partial_value = jnp.einsum(
        "rlf,ldf->rld", grad_gate, gate_weight, preferred_element_type=jnp.float32
    )
    partial_value = partial_value + jnp.einsum(
        "rlf,ldf->rld", grad_up, up_weight, preferred_element_type=jnp.float32
    )
    slot_grad = lax.psum_scatter(
        partial_value.astype(jnp.bfloat16), "etp", scatter_dimension=2, tiled=True
    ).astype(jnp.float32)
    weight_sum = of_everyone(weight_part.astype(jnp.bfloat16), "etp").astype(jnp.float32)
    slot_grad = slot_grad.astype(jnp.bfloat16).reshape(groups, capacity, per_group, half_width)
    slot_dw = weight_sum.astype(jnp.bfloat16).reshape(groups, capacity, per_group)
    returned, returned_weight = (
        lax.all_to_all(slot_grad, "expert", split_axis=0, concat_axis=0, tiled=True),
        lax.all_to_all(slot_dw, "expert", split_axis=0, concat_axis=0, tiled=True),
    )
    gathered = jnp.take(returned.reshape(-1, half_width), flat_slot, axis=0)
    grad_tokens = jnp.sum(gathered.astype(jnp.float32), axis=1).astype(jnp.bfloat16)
    grad_combine = jnp.take(returned_weight.reshape(-1), flat_slot, axis=0)
    return (grad_tokens, grad_combine)


def solution(mesh):
    in_specs = (
        P("expert", "etp"),
        P("expert", None),
        P("expert", None),
        P(None, "expert", "etp"),
        P(None, "expert", "etp"),
        P("expert", None, "etp"),
        P("expert", None, "etp"),
        P("expert", "etp", None),
    )
    out_specs = (P("expert", "etp"), P("expert", None))
    return jax.shard_map(
        on_device, mesh=mesh, in_specs=in_specs, out_specs=out_specs, check_vma=False
    )
```

profile of v0, /device:TPU:34, one launch (start us, length us, event | category | flops | bytes accessed | tf_op | source)
XLA Modules:
  0.0 432.2 jit_solution(15667458970925996139)
XLA Ops:
  7.2 0.8 copy.92
  8.4 2.4 select_reduce_fusion
  11.0 4.3 scatter_custom_fusion
  15.4 0.5 broadcast_in_dim.69
  16.4 1.1 concatenate.7
  17.5 10.6 %gather_fusion.1 = bf16[2048,1792]{1,0:T(8,128)(2,1)} fusion(bf16[129,1792]{1,0:T(8,128)(2,1)S(1)} %concatenate.7, s32[2048]{0:T(1024)S(1)} %get-tuple-element.17), kind=kCustom, calls=%fused_computation.1 | custom fusion | bytes 14688256 | tf_op jit(solution)/shard_map/jit(_take)/gather | solution.py:48
  28.1 15.0 %gather.20 = bf16[64,16,2,1792]{3,2,1,0:T(2,128)(2,1)} reshape(bf16[2048,1792]{1,0:T(8,128)(2,1)} %gather_fusion.1) | data formatting | bytes 14680064 | tf_op jit(solution)/shard_map/jit(_take)/gather | solution.py:48
  43.1 4.8 %copy_select_fusion = bf16[64,16,2,1792]{3,1,2,0:T(8,128)(2,1)S(1)} fusion(bf16[64,16,2,1792]{3,2,1,0:T(2,128)(2,1)} %gather.20, pred[64,16,2]{1,2,0:T(4,128)(4,1)S(1)} %copy.101), kind=kLoop, calls=%fused_computation.7 | loop fusion | flops 3670016 | bytes 14682112 | tf_op jit(solution)/shard_map/jit(_take)/select_n | solution.py:48
  47.9 95.6 %all_to_all.25 = bf16[64,16,2,1792]{3,1,2,0:T(8,128)(2,1)S(1)} all-to-all(bf16[64,16,2,1792]{3,1,2,0:T(8,128)(2,1)S(1)} %copy_select_fusion), channel_id=1, replica_groups=mesh['expert'=64,'etp'=2] {'expert'}, dimensions={0} | all-to-all | bytes 14680064 | tf_op jit(solution)/shard_map/all_to_all | solution.py:52
  143.5 3.5 copy.103
  147.0 0.7 copy-done.2
  147.9 13.1 %gather_fusion = bf16[2048]{0:T(1024)(128)(2,1)S(1)} fusion(bf16[1025]{0:T(1024)(128)(2,1)S(1)} %pad_maximum_fusion, s32[2048]{0:T(1024)S(1)} %get-tuple-element.16), kind=kCustom, calls=%fused_computation | custom fusion | bytes 16384 | tf_op jit(solution)/shard_map/jit(_take)/gather | solution.py:46
  161.6 1.1 copy.98
  162.7 6.5 %all-to-all-start = ((bf16[64,16,2]{1,2,0:T(2,128)(2,1)}), bf16[64,16,2]{1,2,0:T(2,128)(2,1)S(1)}, u32[]{:S(2)}, u32[]{:S(2)}) async-start(bf16[64,16,2]{1,2,0:T(2,128)(2,1)} %copy.98), calls=%async_computation | async-start | bytes 65536 | tf_op jit(solution)/shard_map/all_to_all | solution.py:53
  169.4 4.7 %copy.105 = bf16[1024,2,512]{0,2,1:T(8,128)(2,1)} copy(bf16[1024,2,512]{2,1,0:T(2,128)(2,1)S(1)} %copy-done) | data formatting | bytes 4194304 | tf_op args[3]
  174.2 6.3 %copy.104 = bf16[1024,2,512]{0,2,1:T(8,128)(2,1)} copy(bf16[1024,2,512]{2,1,0:T(2,128)(2,1)} %param.12) | data formatting | bytes 4194304 | tf_op args[4]
  180.8 15.4 %fusion.4 = (bf16[1024,2]{0,1:T(2,128)(2,1)S(1)}, f32[2,1024,512]{1,2,0:T(8,128)}) fusion(bf16[1024,2,512]{0,2,1:T(8,128)(2,1)} %copy.104, bf16[1024,2,512]{0,2,1:T(8,128)(2,1)S(1)} %copy-done.1, bf16[1024,2,3584]{2,0,1:T(8,128)(2,1)} %all-gather.2.cloned.1.call-done, bf16[2,512,3584]{2,1,0:T(8,128)(2,1)} %param.15), kind=kOutput, calls=%fused_computation.16 | convolution fusion | flops 7525627904 | bytes 30412800 | tf_op jit(solution)/shard_map/rld,lfd->rlf/dot_general | solution.py:58
  196.2 18.9 %fusion.10 = f32[2,1024,3584]{2,1,0:T(8,128)} fusion(bf16[2,3584,512]{2,1,0:T(8,128)(2,1)} %param.13, bf16[1024,2,512]{0,2,1:T(8,128)(2,1)} %copy.104, bf16[1024,2,512]{0,2,1:T(8,128)(2,1)S(1)} %copy-done.1, f32[2,1024,512]{1,2,0:T(8,128)} %get-tuple-element.19, f32[1024,2]{0,1:T(2,128)S(1)} %reshape.107), kind=kOutput, calls=%fused_computation.26 | convolution fusion | flops 7529824256 | bytes 45096960 | tf_op jit(solution)/shard_map/rlf,ldf->rld/dot_general | solution.py:71
  215.1 20.6 %fusion = bf16[1024,2,3584]{2,0,1:T(8,128)(2,1)} fusion(f32[2,1024,3584]{2,1,0:T(8,128)} %fusion.10, bf16[2,3584,512]{2,1,0:T(8,128)(2,1)} %param.14, f32[2,1024,512]{1,2,0:T(8,128)} %get-tuple-element.19, f32[1024,2]{0,1:T(2,128)S(1)} %reshape.107, bf16[1024,2,512]{0,2,1:T(8,128)(2,1)S(1)} %copy-done.1), kind=kOutput, calls=%fused_computation.6 | convolution fusion | flops 7539261440 | bytes 57679872 | tf_op jit(solution)/shard_map/rlf,ldf->rld/dot_general | solution.py:74
  235.7 3.7 all_to_all.26
  239.6 0.7 copy.110
  240.2 10.3 %all-to-all-start.4 = ((bf16[64,16,2]{1,2,0:T(2,128)(2,1)}), bf16[64,16,2]{1,2,0:T(2,128)(2,1)S(1)}, u32[]{:S(2)}, u32[]{:S(2)}) async-start(bf16[64,16,2]{1,2,0:T(2,128)(2,1)} %copy.110), calls=%async_computation.5 | async-start | bytes 65536 | tf_op jit(solution)/shard_map/all_to_all | solution.py:85
  250.6 10.4 %reduce-scatter.2.cloned.1.call-done = bf16[1024,2,1792]{2,0,1:T(8,128)(2,1)} async-done(((bf16[1024,2,3584]{2,0,1:T(8,128)(2,1)}), bf16[1024,2,1792]{2,0,1:T(8,128)(2,1)}) %reduce-scatter.2.cloned.1.call-update) | async-done | bytes 7340048 | tf_op jit(solution)/shard_map/reduce_scatter | solution.py:77
  261.0 7.2 %copy.108 = bf16[64,16,2,1792]{3,1,2,0:T(8,128)(2,1)} copy(bf16[64,16,2,1792]{3,1,0,2:T(8,128)(2,1)} %bitcast.30) | data formatting | bytes 14680064 | tf_op jit(solution)/shard_map/reshape | solution.py:81
  268.2 10.5 %all-to-all-start.2 = ((bf16[64,16,2,1792]{3,1,2,0:T(8,128)(2,1)}), bf16[64,16,2,1792]{3,1,2,0:T(8,128)(2,1)}, u32[]{:S(2)}, u32[]{:S(2)}) async-start(bf16[64,16,2,1792]{3,1,2,0:T(8,128)(2,1)} %copy.108), calls=%async_computation.3 | async-start | bytes 14680064 | tf_op jit(solution)/shard_map/all_to_all | solution.py:84
  279.6 6.8 %gather_fusion.3 = bf16[1024]{0:T(1024)(128)(2,1)S(1)} fusion(bf16[2048]{0:T(1024)(128)(2,1)S(1)} %reshape.106, s32[1024]{0:T(1024)S(1)} %broadcast_clamp_fusion.1), kind=kCustom, calls=%fused_computation.3 | custom fusion | bytes 8192 | tf_op jit(solution)/shard_map/jit(_take)/gather | solution.py:89
  286.5 0.7 copy.112
  287.2 94.1 %all-to-all-done.2 = bf16[64,16,2,1792]{3,1,2,0:T(8,128)(2,1)} async-done(((bf16[64,16,2,1792]{3,1,2,0:T(8,128)(2,1)}), bf16[64,16,2,1792]{3,1,2,0:T(8,128)(2,1)}, u32[]{:S(2)}, u32[]{:S(2)}) %all-to-all-start.2) | async-done | bytes 7340064 | tf_op jit(solution)/shard_map/all_to_all | solution.py:84
  381.3 11.7 %copy.109 = bf16[64,16,2,1792]{3,2,1,0:T(2,128)(2,1)} copy(bf16[64,16,2,1792]{3,1,2,0:T(8,128)(2,1)} %all-to-all-done.2) | data formatting | bytes 14680064 | tf_op jit(solution)/shard_map/all_to_all | solution.py:84
  393.1 15.6 %reshape.104 = bf16[2048,1792]{1,0:T(8,128)(2,1)} reshape(bf16[64,16,2,1792]{3,2,1,0:T(2,128)(2,1)} %copy.109) | data formatting | bytes 14680064 | tf_op jit(solution)/shard_map/reshape | solution.py:87
  408.6 12.0 %gather_fusion.2 = bf16[1024,1792]{1,0:T(8,128)(2,1)} fusion(bf16[2048,1792]{1,0:T(8,128)(2,1)} %reshape.104, s32[1024]{0:T(1024)S(1)} %broadcast_clamp_fusion.1), kind=kCustom, calls=%fused_computation.2 | custom fusion | bytes 7344128 | tf_op jit(solution)/shard_map/jit(_take)/gather | solution.py:87
  420.6 4.7 %fusion.9 = bf16[128,1792]{1,0:T(8,128)(2,1)} fusion(bf16[1024,1792]{1,0:T(8,128)(2,1)} %gather_fusion.2, pred[128,8]{1,0:T(8,128)(4,1)S(1)} %get-tuple-element.13), kind=kLoop, calls=%fused_computation.25 | loop fusion | flops 3440640 | bytes 4129792 | tf_op jit(solution)/shard_map/reduce_sum | solution.py:88
  (39 shorter events, 3.6 us)
Async XLA Ops:
  7.2 173.6 %all-gather.2.cloned.1.call-start = ((), (), s32[]{:S(2)}) async-start(), calls=%async_computation.6 | async-start | bytes 22020096 | tf_op jit(solution)/shard_map/all_gather | solution.py:55
  147.0 0.7 copy-start.2
  147.7 21.7 %copy-start = (bf16[1024,2,512]{2,1,0:T(2,128)(2,1)S(1)}, bf16[1024,2,512]{2,1,0:T(2,128)(2,1)}, u32[]{:S(2)}) copy-start(bf16[1024,2,512]{2,1,0:T(2,128)(2,1)} %param.11) | copy-start | bytes 6291460
  162.7 17.8 %all-to-all-start = ((bf16[64,16,2]{1,2,0:T(2,128)(2,1)}), bf16[64,16,2]{1,2,0:T(2,128)(2,1)S(1)}, u32[]{:S(2)}, u32[]{:S(2)}) async-start(bf16[64,16,2]{1,2,0:T(2,128)(2,1)} %copy.98), calls=%async_computation | async-start | bytes 65536 | tf_op jit(solution)/shard_map/all_to_all | solution.py:53
  169.2 91.8 %reduce-scatter.2.cloned.1.call-start = ((), (), s32[]{:S(2)}) async-start(), calls=%async_computation.7 | async-start | bytes 22020096 | tf_op jit(solution)/shard_map/reduce_scatter | solution.py:77
  174.2 6.6 %copy-start.1 = (bf16[1024,2,512]{0,2,1:T(8,128)(2,1)S(1)}, bf16[1024,2,512]{0,2,1:T(8,128)(2,1)}, u32[]{:S(2)}) copy-start(bf16[1024,2,512]{0,2,1:T(8,128)(2,1)} %copy.105) | copy-start | bytes 6291460
  240.2 28.0 %all-to-all-start.4 = ((bf16[64,16,2]{1,2,0:T(2,128)(2,1)}), bf16[64,16,2]{1,2,0:T(2,128)(2,1)S(1)}, u32[]{:S(2)}, u32[]{:S(2)}) async-start(bf16[64,16,2]{1,2,0:T(2,128)(2,1)} %copy.110), calls=%async_computation.5 | async-start | bytes 65536 | tf_op jit(solution)/shard_map/all_to_all | solution.py:85
  268.2 113.1 %all-to-all-start.2 = ((bf16[64,16,2,1792]{3,1,2,0:T(8,128)(2,1)}), bf16[64,16,2,1792]{3,1,2,0:T(8,128)(2,1)}, u32[]{:S(2)}, u32[]{:S(2)}) async-start(bf16[64,16,2,1792]{3,1,2,0:T(8,128)(2,1)} %copy.108), calls=%async_computation.3 | async-start | bytes 14680064 | tf_op jit(solution)/shard_map/all_to_all | solution.py:84
Sparse Core Ops, SparseCore 0:
  147.2 27.2 all-gather.1
  235.8 25.1 reduce-scatter.1
where the time goes:
time: 434 us; the launch traced here: 432 us
  local copies, waits for them, and re-layouts  119 us (27%)
  waiting for transfers between devices  105 us (24%)
  blocking collectives  99.3 us (23%)
  matrix products  54.9 us (13%)
  starting transfers between devices  27.6 us (6%)
  between operations  14.2 us (3%)
  other arithmetic  12.5 us (3%)
    all_to_all x1, blocking collectives, on_device(): lax.all_to_all(outgoing, 'expert', split_axis=0, concat_axis=0, tiled=True)  95.6 us
    all_to_all x1, waiting for transfers between devices, on_device(): lax.all_to_all(slot_grad, 'expert', split_axis=0, concat_axis=0, tiled=True)  94.1 us
    gather x2, local copies, waits for them, and re-layouts, on_device(): jnp.take(padded, source_token, axis=0)  25.7 us
    dot_general x1, matrix products, on_device(): jnp.einsum('rlf,ldf->rld', grad_up, up_weight, preferred_element_type=jnp...  20.6 us
    dot_general x1, matrix products, on_device(): jnp.einsum('rlf,ldf->rld', grad_gate, gate_weight, preferred_element_type...  18.9 us
    reshape x1, local copies, waits for them, and re-layouts, on_device(): gathered = jnp.take(returned.reshape(-1, half_width), flat_slot, axis=0)  15.6 us
    dot_general x1, matrix products, on_device(): jnp.einsum('rld,lfd->rlf', slot_rows, down_weight, preferred_element_type...  15.4 us
    unnamed x11, local copies, waits for them, and re-layouts  13.3 us
  transfers between devices with their start and end apart: 5, of which 2 were waited for; matrix products, arithmetic and copies ran while one was open for 10% of the time, Pallas kernels for 0%

commit v1 on v0

v1 whole, which is shorter than its diff:
```python
import functools

import jax
import jax.numpy as jnp
from jax import lax
from jax.experimental import pallas as pl
from jax.experimental.pallas import tpu as pltpu
from jax.sharding import PartitionSpec as P

BOTH = ("expert", "etp")
CHUNKS = 1
F32 = jnp.float32
BF16 = jnp.bfloat16


def places(ids_ref, experts):
    top, tokens = ids_ref.shape
    ids = ids_ref[...]
    names = lax.broadcasted_iota(jnp.int32, (experts, tokens), 0)
    hits = [ids[k:k + 1, :] == names for k in range(top)]
    member = functools.reduce(jnp.logical_or, hits)
    earlier = (
        lax.broadcasted_iota(jnp.int32, (tokens, tokens), 0)
        < lax.broadcasted_iota(jnp.int32, (tokens, tokens), 1)
    )
    before = jnp.dot(
        member.astype(F32).astype(BF16), earlier.astype(F32).astype(BF16),
        preferred_element_type=F32,
    )
    return hits, jnp.where(member, before, -1.0)


def pack_kernel(first, ids_ref, tokens_ref, out_ref, place_ref):
    step = pl.program_id(0)
    batch, depth, _ = out_ref.shape
    experts = place_ref.shape[0]

    @pl.when(step == 0)
    def _():
        place_ref[...] = places(ids_ref, experts)[1]

    place = place_ref[pl.ds(step * batch, batch), :]
    slots = first + lax.broadcasted_iota(jnp.int32, (batch, depth, place.shape[1]), 1)
    pick = (place[:, None, :] == slots.astype(F32)).astype(F32)
    pick = pick.reshape(batch * depth, place.shape[1]).astype(BF16)
    out = jnp.dot(pick, tokens_ref[...], preferred_element_type=F32)
    out_ref[...] = out.astype(BF16).reshape(out_ref.shape)


def pack(ids, tokens, experts, first, depth):
    count, width = tokens.shape
    batch = 256 // depth
    return pl.pallas_call(
        functools.partial(pack_kernel, first),
        grid=(experts // batch,),
        in_specs=[
            pl.BlockSpec(ids.shape, lambda i: (0, 0)),
            pl.BlockSpec(tokens.shape, lambda i: (0, 0)),
        ],
        out_specs=pl.BlockSpec((batch, depth, width), lambda i: (i, 0, 0)),
        out_shape=jax.ShapeDtypeStruct((experts, depth, width), BF16),
        scratch_shapes=[pltpu.VMEM((experts, count), F32)],
        name=f"pack_{first}",
    )(ids, tokens)


def expert_kernel(
    which_ref, arrived_ref, gate_own, gate_other, up_own, up_other,
    down_mine, down_sent, gatew_mine, gatew_sent, upw_mine, upw_sent,
    back_ref, weight_ref, down_v, mix_v, sems,
):
    step = pl.program_id(0)
    half = down_v.shape[0] // 2
    mine = which_ref[0]
    copies = [
        pltpu.make_async_copy(down_mine.at[mine], down_v.at[0:half], sems.at[0]),
        pltpu.make_async_copy(down_sent, down_v.at[half:2 * half], sems.at[1]),
        pltpu.make_async_copy(gatew_mine.at[mine], mix_v.at[:, 0:half], sems.at[2]),
        pltpu.make_async_copy(gatew_sent, mix_v.at[:, half:2 * half], sems.at[3]),
        pltpu.make_async_copy(upw_mine.at[mine], mix_v.at[:, 2 * half:3 * half], sems.at[4]),
        pltpu.make_async_copy(upw_sent, mix_v.at[:, 3 * half:4 * half], sems.at[5]),
    ]

    @pl.when(step == 0)
    def _():
        for copy in copies:
            copy.start()
        copies[0].wait()
        copies[1].wait()

    groups, halves, depth, width = arrived_ref.shape
    rows = groups * depth
    dims = (((1,), (1,)), ((), ()))
    grad = None
    for h in range(halves):
        part = lax.dot_general(
            arrived_ref[:, h].reshape(rows, width),
            down_v[:, h * width:(h + 1) * width], dims, preferred_element_type=F32,
        )
        grad = part if grad is None else grad + part
    mixed = []
    total = None
    for i, (gate_ref, up_ref) in enumerate(((gate_own, up_own), (gate_other, up_other))):
        g = grad[:, i * half:(i + 1) * half]
        gate = gate_ref[...].reshape(rows, half).astype(F32)
        up = up_ref[...].reshape(rows, half).astype(F32)
        s = jax.nn.sigmoid(gate)
        act = gate * s
        g_act = g * act
        product = g_act * up
        mixed.append(((g * up) * (s * (1.0 + gate * (1.0 - s)))).astype(BF16))
        mixed.append(g_act.astype(BF16))
        for j in range(half // 128):
            term = product[:, j * 128:(j + 1) * 128]
            total = term if total is None else total + term
    weight_ref[...] = jnp.sum(total.T, axis=0, keepdims=True).reshape(weight_ref.shape)

    @pl.when(step == 0)
    def _():
        for copy in copies[2:]:
            copy.wait()

    joined = jnp.concatenate([mixed[0], mixed[2], mixed[1], mixed[3]], axis=1)
    for h in range(halves):
        out = lax.dot_general(
            joined, mix_v[h * width:(h + 1) * width, :], dims, preferred_element_type=F32,
        )
        back_ref[:, h] = out.astype(BF16).reshape(groups, depth, width)


def expert_step(mine, arrived, saved, weights, first):
    groups, halves, depth, width = arrived.shape
    half = saved[0].shape[-1]
    batch = 256 // depth
    steps = groups // batch
    part = first // depth

    saved_spec = pl.BlockSpec((batch, depth, half), lambda i, s: (i, part, 0))
    hbm = pl.BlockSpec(memory_space=pl.ANY)
    return pl.pallas_call(
        expert_kernel,
        grid_spec=pltpu.PrefetchScalarGridSpec(
            num_scalar_prefetch=1,
            grid=(steps,),
            in_specs=[
                pl.BlockSpec((batch, halves, depth, width), lambda i, s: (i, 0, 0, 0)),
                saved_spec, saved_spec, saved_spec, saved_spec,
                hbm, hbm, hbm, hbm, hbm, hbm,
            ],
            out_specs=[
                pl.BlockSpec((batch, halves, depth, width), lambda i, s: (i, 0, 0, 0)),
                pl.BlockSpec((1, 1, batch * depth), lambda i, s: (i, 0, 0)),
            ],
            scratch_shapes=[
                pltpu.VMEM((2 * half, halves * width), BF16),
                pltpu.VMEM((halves * width, 4 * half), BF16),
                pltpu.SemaphoreType.DMA((6,)),
            ],
        ),
        out_shape=[
            jax.ShapeDtypeStruct((groups, halves, depth, width), BF16),
            jax.ShapeDtypeStruct((steps, 1, batch * depth), F32),
        ],
        compiler_params=pltpu.CompilerParams(vmem_limit_bytes=58 * 1024 * 1024),
        name=f"expert_{first}",
    )(mine, arrived, *saved, *weights)


def merge_kernel(chunks, ids_ref, combine_ref, *refs):
    back_refs, dw_refs = refs[:chunks], refs[chunks:2 * chunks]
    tokens_ref, grad_combine_ref, place_ref, share_ref, sum_ref = refs[2 * chunks:]
    step = pl.program_id(0)
    batch, depth, width = back_refs[0].shape
    experts, count = place_ref.shape
    top = ids_ref.shape[0]

    @pl.when(step == 0)
    def _():
        hits, place = places(ids_ref, experts)
        place_ref[...] = place
        share = jnp.zeros((experts, count), F32)
        for k in range(top):
            share = share + jnp.where(hits[k], combine_ref[k:k + 1, :].astype(F32), 0.0)
        share_ref[...] = share
        sum_ref[...] = jnp.zeros_like(sum_ref)
        found = jnp.zeros((experts, count), F32)
        for n in range(chunks):
            for c in range(depth):
                value = dw_refs[n][:, c:c + 1].astype(F32)
                found = found + jnp.where(place == float(n * depth + c), value, 0.0)
        rows = [
            jnp.sum(jnp.where(hits[k], found, 0.0), axis=0, keepdims=True) for k in range(top)
        ]
        grad_combine_ref[...] = jnp.concatenate(rows, axis=0).astype(BF16)

    here = pl.ds(step * batch, batch)
    place, share = place_ref[here, :], share_ref[here, :]
    for n in range(chunks):
        slots = n * depth + lax.broadcasted_iota(jnp.int32, (batch, depth, count), 1)
        take = jnp.where(place[:, None, :] == slots.astype(F32), share[:, None, :], 0.0)
        take = take.reshape(batch * depth, count)
        sum_ref[...] += jnp.dot(
            take.T.astype(BF16), back_refs[n][...].reshape(batch * depth, width),
            preferred_element_type=F32,
        )

    @pl.when(step == pl.num_programs(0) - 1)
    def _():
        tokens_ref[...] = sum_ref[...].astype(BF16)


def merge(ids, combine, backs, dws):
    experts, depth, width = backs[0].shape
    top, count = ids.shape
    chunks = len(backs)
    batch = 256 // depth // chunks
    whole = lambda x: pl.BlockSpec(x.shape, lambda i: (0, 0))
    return pl.pallas_call(
        functools.partial(merge_kernel, chunks),
        grid=(experts // batch,),
        in_specs=[whole(ids), whole(combine)]
        + [pl.BlockSpec((batch, depth, width), lambda i: (i, 0, 0))] * chunks
        + [whole(x) for x in dws],
        out_specs=[
            pl.BlockSpec((count, width), lambda i: (0, 0)),
            pl.BlockSpec((top, count), lambda i: (0, 0)),
        ],
        out_shape=[
            jax.ShapeDtypeStruct((count, width), BF16),
            jax.ShapeDtypeStruct((top, count), BF16),
        ],
        scratch_shapes=[
            pltpu.VMEM((experts, count), F32),
            pltpu.VMEM((experts, count), F32),
            pltpu.VMEM((count, width), F32),
        ],
        name="merge",
    )(ids, combine, *backs, *dws)


def on_device(
    grad_out, combine, expert_ids, saved_gate, saved_up, gate_weight, up_weight, down_weight
):
    groups = lax.axis_size("expert")
    halves = lax.axis_size("etp")
    mine = lax.axis_index("etp")
    experts = groups * gate_weight.shape[0]
    width = grad_out.shape[1]
    capacity = saved_gate.shape[0] // groups
    depth = capacity // CHUNKS
    ids, shares = expert_ids.T, combine.T

    swap = [(0, 1), (1, 0)]

    def both(x, axis):
        own = lax.dynamic_index_in_dim(x, mine, axis, keepdims=False)
        other = lax.dynamic_index_in_dim(x, 1 - mine, axis, keepdims=False)
        return own, lax.ppermute(other, "etp", swap)

    arrivals = []
    for n in range(CHUNKS):
        outgoing = pack(ids, grad_out, experts, n * depth, depth)
        arrivals.append(
            lax.all_to_all(outgoing, BOTH, split_axis=0, concat_axis=0, tiled=True)
        )
    weights = []
    for x in (down_weight, gate_weight, up_weight):
        other = lax.dynamic_index_in_dim(x, 1 - mine, 0, keepdims=False)
        weights += [x, lax.ppermute(other, "etp", swap)]
    saved = []
    for x in (saved_gate, saved_up):
        for y in both(x, 1):
            saved.append(y.reshape(groups, capacity, y.shape[-1]))

    returned, returned_dw = [], []
    for n in range(CHUNKS):
        back, dw = expert_step(
            mine.reshape(1), arrivals[n].reshape(groups, halves, depth, width),
            saved, weights, n * depth,
        )
        dw = dw.reshape(groups, 1, depth).astype(BF16)
        dw = jnp.broadcast_to(dw, (groups, halves, depth)).reshape(experts, depth)
        returned_dw.append(lax.all_to_all(dw, BOTH, split_axis=0, concat_axis=0, tiled=True))
        returned.append(
            lax.all_to_all(
                back.reshape(groups * halves, depth, width), BOTH,
                split_axis=0, concat_axis=0, tiled=True,
            )
        )
    grad_tokens, grad_combine = merge(ids, shares, returned, returned_dw)
    return grad_tokens, grad_combine.T


def solution(mesh):
    in_specs = (
        P("expert", "etp"),
        P("expert", None),
        P("expert", None),
        P(None, "expert", "etp"),
        P(None, "expert", "etp"),
        P("expert", None, "etp"),
        P("expert", None, "etp"),
        P("expert", "etp", None),
    )
    out_specs = (P("expert", "etp"), P("expert", None))
    return jax.shard_map(
        on_device, mesh=mesh, in_specs=in_specs, out_specs=out_specs, check_vma=False
    )
```

time: 434 us -> 269 us (0.62)
  local copies, waits for them, and re-layouts: 119 us -> 25.7 us
  blocking collectives: 99.3 us -> 18.7 us
  matrix products: 54.9 us -> 0 us
  Pallas kernels: 0 us -> 48.8 us
  waiting for transfers between devices: 105 us -> 151 us
  between operations: 14.2 us -> 0.73 us
  other arithmetic: 12.5 us -> 0.71 us
  starting transfers between devices: 27.6 us -> 19.7 us
    all_to_all x2 -> x1, blocking collectives: 99.3 us -> 18.7 us  [on_device(): lax.all_to_all(dw, BOTH, split_axis=0, concat_axis=0, tiled=True)]
    gather x6 -> x0, local copies, waits for them, and re-layouts: 57.6 us -> none  [the longest x2 25.7 us: on_device(): jnp.take(padded, source_token, axis=0)]
    all_to_all x3 -> x2, waiting for transfers between devices: 94.1 us -> 150 us  [the longest x1 88 us: on_device(): lax.all_to_all(back.reshape(groups * halves, depth, width), BOTH, split_a...]
    dot_general x3 -> x0, matrix products: 54.9 us -> none  [the longest x1 20.6 us: on_device(): jnp.einsum('rlf,ldf->rld', grad_up, up_weight, preferred_element_type=jnp...]
    pallas_call x0 -> x3, Pallas kernels: none -> 48.8 us  [the longest x1 33.9 us: expert_step(): pl.pallas_call(expert_kernel, grid_spec=pltpu.PrefetchScalarGridSpec(num_...]
    reshape x7 -> x0, local copies, waits for them, and re-layouts: 24.1 us -> none  [the longest x1 15.6 us: on_device(): gathered = jnp.take(returned.reshape(-1, half_width), flat_slot, axis=0)]
    all_to_all x4 -> x2, local copies, waits for them, and re-layouts: 15.8 us -> 0.67 us  [on_device(): lax.all_to_all(dw, BOTH, split_axis=0, concat_axis=0, tiled=True)]
    squeeze x0 -> x3, local copies, waits for them, and re-layouts: none -> 10.5 us  [on_device(): other = lax.dynamic_index_in_dim(x, 1 - mine, 0, keepdims=False)]
  transfers between devices with their start and end apart: 5 -> 7, of which waited for: 2 -> 3; matrix products, arithmetic and copies ran while one was open for 10% -> 9% of each run, Pallas kernels for 0% -> 0%
where the time goes in v1:
time: 269 us; the launch traced here: 265 us
  waiting for transfers between devices  151 us (56%)
  Pallas kernels  48.8 us (18%)
  local copies, waits for them, and re-layouts  25.7 us (10%)
  starting transfers between devices  19.7 us (7%)
  blocking collectives  18.7 us (7%)
    all_to_all x1, waiting for transfers between devices, on_device(): lax.all_to_all(back.reshape(groups * halves, depth, width), BOTH, split_a...  88 us
    all_to_all x1, waiting for transfers between devices, on_device(): lax.all_to_all(outgoing, BOTH, split_axis=0, concat_axis=0, tiled=True)  62.3 us
    pallas_call x1, Pallas kernels, expert_step(): pl.pallas_call(expert_kernel, grid_spec=pltpu.PrefetchScalarGridSpec(num_...  33.9 us
    all_to_all x1, blocking collectives, on_device(): lax.all_to_all(dw, BOTH, split_axis=0, concat_axis=0, tiled=True)  18.7 us
    all_to_all x1, starting transfers between devices, on_device(): lax.all_to_all(outgoing, BOTH, split_axis=0, concat_axis=0, tiled=True)  10.6 us
    squeeze x3, local copies, waits for them, and re-layouts, on_device(): other = lax.dynamic_index_in_dim(x, 1 - mine, 0, keepdims=False)  10.5 us
    dynamic_slice x1, local copies, waits for them, and re-layouts, both(): other = lax.dynamic_index_in_dim(x, 1 - mine, axis, keepdims=False)  10.3 us
    pallas_call x1, Pallas kernels, merge(): pl.pallas_call(functools.partial(merge_kernel, chunks), grid=(experts //...  7.97 us
  transfers between devices with their start and end apart: 7, of which 3 were waited for; matrix products, arithmetic and copies ran while one was open for 9% of the time, Pallas kernels for 0%

profile of v1, /device:TPU:34, one launch (start us, length us, event | category | flops | bytes accessed | tf_op | source)
XLA Modules:
  0.0 265.3 jit_solution(1780569795072168326)
XLA Ops:
  0.6 7.0 %pack_0.1 = bf16[128,16,1792]{2,1,0:T(8,128)(2,1)} custom-call(s32[8,128]{1,0:T(8,128)} %bitcast.36, bf16[128,1792]{1,0:T(8,128)(2,1)} %tokens_ref.1), custom_call_target="tpu_custom_call" | custom-call | tf_op jit(solution)/shard_map/pack_0/pallas_call | solution.py:53
  7.6 10.6 %all-to-all-start = ((bf16[128,16,1792]{2,1,0:T(8,128)(2,1)}), bf16[128,16,1792]{2,1,0:T(8,128)(2,1)}, u32[]{:S(2)}, u32[]{:S(2)}) async-start(bf16[128,16,1792]{2,1,0:T(8,128)(2,1)} %pack_0.1), calls=%async_computation | async-start | bytes 14680064 | tf_op jit(solution)/shard_map/all_to_all | solution.py:264
  18.3 0.0 copy-start
  18.3 4.3 %dynamic-slice_bitcast_fusion.2 = bf16[512,3584]{1,0:T(8,128)(2,1)} fusion(bf16[2,512,3584]{2,1,0:T(8,128)(2,1)} %down_mine.1, s32[]{:T(128)S(6)} %select_n.15), kind=kLoop, calls=%fused_computation.2 | loop fusion | bytes 7340036 | tf_op jit(solution)/shard_map/jit(dynamic_index_in_dim)/squeeze | solution.py:268
  22.6 0.1 collective-permute-start.2
  22.7 1.1 copy-done
  23.8 2.0 dynamic-slice_bitcast_fusion
  25.8 0.1 collective-permute-start.4
  25.9 4.2 %dynamic-slice_bitcast_fusion.1 = bf16[3584,512]{1,0:T(8,128)(2,1)} fusion(bf16[2,3584,512]{2,1,0:T(8,128)(2,1)} %gatew_mine.1, s32[]{:T(128)S(6)} %select_n.15), kind=kLoop, calls=%fused_computation.1 | loop fusion | bytes 7340036 | tf_op jit(solution)/shard_map/jit(dynamic_index_in_dim)/squeeze | solution.py:268
  30.1 0.5 collective-permute-start.3
  30.6 10.3 %constant_dynamic-slice_fusion = (bf16[1024,1,512]{2,1,0:T(2,128)(2,1)S(1)}, bf16[1024,1,512]{2,1,0:T(2,128)(2,1)S(1)}, bf16[1024,1,512]{2,1,0:T(2,128)(2,1)S(1)}, bf16[1024,1,512]{2,1,0:T(2,128)(2,1)S(1)}) fusion(bf16[1024,2,512]{2,1,0:T(2,128)(2,1)S(1)} %copy-done.1, s32[]{:T(128)S(6)} %select_n.15, s32[]{:T(128)S(6)} %select_n.14, ...), kind=kLoop, calls=%fused_computation.7 | loop fusion | bytes 8388616 | tf_op jit(solution)/shard_map/jit(dynamic_index_in_dim)/dynamic_slice | solution.py:257
  40.8 0.3 copy.34
  41.1 0.1 collective-permute-start
  41.3 0.3 copy.33
  41.5 0.7 collective-permute-start.1
  42.3 1.2 copy.28
  43.5 1.3 copy.26
  44.8 0.0 collective-permute-done
  44.8 0.6 collective-permute-done.1
  45.4 0.0 collective-permute-done.2.down_sent
  45.4 0.0 collective-permute-done.4.upw_sent
  45.4 0.0 collective-permute-done.3.gatew_sent
  45.4 62.3 %all-to-all-done = bf16[128,16,1792]{2,1,0:T(8,128)(2,1)} async-done(((bf16[128,16,1792]{2,1,0:T(8,128)(2,1)}), bf16[128,16,1792]{2,1,0:T(8,128)(2,1)}, u32[]{:S(2)}, u32[]{:S(2)}) %all-to-all-start) | async-done | bytes 7340064 | tf_op jit(solution)/shard_map/all_to_all | solution.py:264
  107.7 33.9 %expert_0.1 = (bf16[64,2,16,1792]{3,2,1,0:T(8,128)(2,1)}, f32[4,1,256]{2,1,0:T(1,128)}) custom-call(s32[1]{0:T(128)} %bitcast.2.which_ref, bf16[64,2,16,1792]{3,2,1,0:T(8,128)(2,1)} %bitcast.3.arrived_ref, bf16[64,16,512]{2,1,0:T(8,128)(2,1)} %bitcast.29, bf16[64,16,512]{2,1,0:T(8,128)(2,1)} %bitcast.30, bf16[64,16,512]{2,1,0:T(8,128)(2,1)} %bitcast.28, ...), custom_call_target="tpu_custom_call" | custom-call | tf_op jit(solution)/shard_map/expert_0/pallas_call | solution.py:140
  141.6 0.7 convert_reduce_fusion
  142.3 0.1 convert_element_type.12
  142.4 0.1 copy.22
  142.4 18.7 %all_to_all.21 = bf16[128,1,16]{2,1,0:T(2,128)(2,1)S(1)} all-to-all(bf16[128,1,16]{2,1,0:T(2,128)(2,1)S(1)} %copy.22), channel_id=1, replica_groups=mesh['expert'=64,'etp'=2] {'expert','etp'}, dimensions={0} | all-to-all | bytes 8192 | tf_op jit(solution)/shard_map/all_to_all | solution.py:283
  161.2 7.5 %all-to-all-start.1 = ((bf16[128,16,1792]{2,1,0:T(8,128)(2,1)}), bf16[128,16,1792]{2,1,0:T(8,128)(2,1)}, u32[]{:S(2)}, u32[]{:S(2)}) async-start(bf16[128,16,1792]{2,1,0:T(8,128)(2,1)} %bitcast.27), calls=%async_computation.1 | async-start | bytes 14680064 | tf_op jit(solution)/shard_map/all_to_all | solution.py:285
  168.7 0.6 copy.35
  169.3 88.0 %all-to-all-done.1.refs_0_ = bf16[128,16,1792]{2,1,0:T(8,128)(2,1)} async-done(((bf16[128,16,1792]{2,1,0:T(8,128)(2,1)}), bf16[128,16,1792]{2,1,0:T(8,128)(2,1)}, u32[]{:S(2)}, u32[]{:S(2)}) %all-to-all-start.1) | async-done | bytes 7340064 | tf_op jit(solution)/shard_map/all_to_all | solution.py:285
  257.3 8.0 %merge.1 = (bf16[128,1792]{1,0:T(8,128)(2,1)}, bf16[8,128]{1,0:T(8,128)(2,1)}) custom-call(s32[8,128]{1,0:T(8,128)} %bitcast.37, bf16[8,128]{1,0:T(8,128)(2,1)} %bitcast.38, bf16[128,16,1792]{2,1,0:T(8,128)(2,1)} %all-to-all-done.1.refs_0_, bf16[128,16]{1,0:T(8,128)(2,1)} %bitcast.34), custom_call_target="tpu_custom_call" | custom-call | tf_op jit(solution)/shard_map/merge/pallas_call | solution.py:218
  (7 shorter events, 0.0 us)
Async XLA Ops:
  7.6 100.0 %all-to-all-start = ((bf16[128,16,1792]{2,1,0:T(8,128)(2,1)}), bf16[128,16,1792]{2,1,0:T(8,128)(2,1)}, u32[]{:S(2)}, u32[]{:S(2)}) async-start(bf16[128,16,1792]{2,1,0:T(8,128)(2,1)} %pack_0.1), calls=%async_computation | async-start | bytes 14680064 | tf_op jit(solution)/shard_map/all_to_all | solution.py:264
  18.3 5.5 %copy-start = (bf16[2,3584,512]{2,1,0:T(8,128)(2,1)S(1)}, bf16[2,3584,512]{2,1,0:T(8,128)(2,1)}, u32[]{:S(2)}) copy-start(bf16[2,3584,512]{2,1,0:T(8,128)(2,1)} %upw_mine.1) | copy-start | bytes 22020100
  22.6 22.8 %collective-permute-start.2 = (bf16[512,3584]{1,0:T(8,128)(2,1)}, bf16[512,3584]{1,0:T(8,128)(2,1)}, u32[]{:S(2)}, u32[]{:S(2)}) collective-permute-start(bf16[512,3584]{1,0:T(8,128)(2,1)} %dynamic-slice_bitcast_fusion.2), channel_id=1, source_target_pairs={{0,1},{1,0},{2,3},{3,2},{4,5},{5,4},{6,7},{7,6},{8,9},{9,8},{10,11... | collective-permute-start | bytes 11010056 | tf_op jit(solution)/shard_map/ppermute | solution.py:269
  25.8 4.8 %copy-start.1 = (bf16[1024,2,512]{2,1,0:T(2,128)(2,1)S(1)}, bf16[1024,2,512]{2,1,0:T(2,128)(2,1)}, u32[]{:S(2)}) copy-start(bf16[1024,2,512]{2,1,0:T(2,128)(2,1)} %param.12) | copy-start | bytes 6291460
  25.8 19.6 %collective-permute-start.4 = (bf16[3584,512]{1,0:T(8,128)(2,1)}, bf16[3584,512]{1,0:T(8,128)(2,1)}, u32[]{:S(2)}, u32[]{:S(2)}) collective-permute-start(bf16[3584,512]{1,0:T(8,128)(2,1)} %dynamic-slice_bitcast_fusion), channel_id=1, source_target_pairs={{0,1},{1,0},{2,3},{3,2},{4,5},{5,4},{6,7},{7,6},{8,9},{9,8},{10,11... | collective-permute-start | bytes 11010056 | tf_op jit(solution)/shard_map/ppermute | solution.py:269
  30.1 15.3 %collective-permute-start.3 = (bf16[3584,512]{1,0:T(8,128)(2,1)}, bf16[3584,512]{1,0:T(8,128)(2,1)}, u32[]{:S(2)}, u32[]{:S(2)}) collective-permute-start(bf16[3584,512]{1,0:T(8,128)(2,1)} %dynamic-slice_bitcast_fusion.1), channel_id=1, source_target_pairs={{0,1},{1,0},{2,3},{3,2},{4,5},{5,4},{6,7},{7,6},{8,9},{9,8},{10,11... | collective-permute-start | bytes 11010056 | tf_op jit(solution)/shard_map/ppermute | solution.py:269
  41.1 3.7 %collective-permute-start = (bf16[1024,512]{1,0:T(8,128)(2,1)S(1)}, bf16[1024,512]{1,0:T(8,128)(2,1)S(1)}, u32[]{:S(2)}, u32[]{:S(2)}) collective-permute-start(bf16[1024,512]{1,0:T(8,128)(2,1)S(1)} %bitcast.32), channel_id=1, source_target_pairs={{0,1},{1,0},{2,3},{3,2},{4,5},{5,4},{6,7},{7,6},{8,9},{9,8},{10,11... | collective-permute-start | bytes 3145736 | tf_op jit(solution)/shard_map/ppermute | solution.py:258
  41.5 3.8 %collective-permute-start.1 = (bf16[1024,512]{1,0:T(8,128)(2,1)S(1)}, bf16[1024,512]{1,0:T(8,128)(2,1)S(1)}, u32[]{:S(2)}, u32[]{:S(2)}) collective-permute-start(bf16[1024,512]{1,0:T(8,128)(2,1)S(1)} %bitcast.33), channel_id=1, source_target_pairs={{0,1},{1,0},{2,3},{3,2},{4,5},{5,4},{6,7},{7,6},{8,9},{9,8},{10,11... | collective-permute-start | bytes 3145736 | tf_op jit(solution)/shard_map/ppermute | solution.py:258
  44.8 62.9 %copy-start.2 = (bf16[1024,512]{1,0:T(8,128)(2,1)}, bf16[1024,512]{1,0:T(8,128)(2,1)S(1)}, u32[]{:S(2)}) copy-start(bf16[1024,512]{1,0:T(8,128)(2,1)S(1)} %collective-permute-done) | copy-start | bytes 3145732
  45.4 62.3 %copy-start.3 = (bf16[1024,512]{1,0:T(8,128)(2,1)}, bf16[1024,512]{1,0:T(8,128)(2,1)S(1)}, u32[]{:S(2)}) copy-start(bf16[1024,512]{1,0:T(8,128)(2,1)S(1)} %collective-permute-done.1) | copy-start | bytes 3145732
  161.2 96.2 %all-to-all-start.1 = ((bf16[128,16,1792]{2,1,0:T(8,128)(2,1)}), bf16[128,16,1792]{2,1,0:T(8,128)(2,1)}, u32[]{:S(2)}, u32[]{:S(2)}) async-start(bf16[128,16,1792]{2,1,0:T(8,128)(2,1)} %bitcast.27), calls=%async_computation.1 | async-start | bytes 14680064 | tf_op jit(solution)/shard_map/all_to_all | solution.py:285

commit v2 on v0

v2 whole, which is shorter than its diff:
```python
import functools

import jax
import jax.numpy as jnp
from jax import lax
from jax.experimental import pallas as pl
from jax.experimental.pallas import tpu as pltpu
from jax.sharding import PartitionSpec as P


BOTH = ("expert", "etp")
SIDE = 4
TOP = 8
LANES = 128
META = 16
BATCH = 2
SEND = (2, 1, 3)
F32 = jnp.float32
BF16 = jnp.bfloat16
WIDE = ((0, 1, 2), (1, 2, 0))
NARROW = ((2, 0, 1), (2, 0, 1))
NT = (((1,), (1,)), ((), ()))


def coords(e):
    return [e // (SIDE * SIDE), (e // SIDE) % SIDE, e % SIDE]


def joined(c):
    return (c[0] * SIDE + c[1]) * SIDE + c[2]


def moved(x, lane, stage, distance):
    pairs = []
    for e in range(SIDE ** 3):
        for core in range(2):
            to = coords(e)
            axis = lane[core][stage]
            to[axis] = (to[axis] - distance) % SIDE
            pairs.append((e * 2 + core, joined(to) * 2 + core))
    return lax.ppermute(x, BOTH, pairs)


def gathered(x, lane, stage):
    got = {q: moved(x, lane, stage, q) for q in SEND}
    return [x, got[1], got[2], got[3]]


def scattered(parts, lane, stage):
    got = {q: moved(parts[-q % SIDE], lane, stage, q) for q in SEND}
    return [parts[0], got[1], got[2], got[3]]


def prepare_kernel(tiles, grad_ref, ids_ref, share_ref, *outs):
    first = 0
    for out, count in zip(outs, tiles):
        for i in range(count):
            column = (first + i) * LANES
            out[i * LANES:(i + 1) * LANES, :] = grad_ref[:, column:column + LANES]
        out[count * LANES:count * LANES + TOP, :] = ids_ref[...].astype(F32).astype(BF16)
        out[count * LANES + TOP:count * LANES + META, :] = share_ref[...]
        first += count


def prepare(grad_out, ids, shares, tiles):
    return pl.pallas_call(
        functools.partial(prepare_kernel, tiles),
        out_shape=[jax.ShapeDtypeStruct((n * LANES + META, LANES), BF16) for n in tiles],
        name="prepare",
    )(grad_out, ids, shares)


def settle(names_ref, metas, place_ref, share_ref=None):
    tokens = metas[0].shape[2]
    experts = 2 * SIDE
    at = lax.broadcasted_iota(jnp.int32, (experts, tokens), 0)
    names = jnp.zeros((experts, tokens), jnp.int32)
    for i in range(experts):
        names = jnp.where(at == i, names_ref[i], names)
    names = names.astype(F32)
    members, weights = [], []
    for i in range(SIDE):
        for j in range(SIDE):
            ids = metas[j][i, 0:TOP, :].astype(F32)
            shares = metas[j][i, TOP:META, :].astype(F32)
            member = jnp.zeros((experts, tokens), F32)
            share = jnp.zeros((experts, tokens), F32)
            for k in range(TOP):
                hit = ids[k:k + 1, :] == names
                member = jnp.where(hit, 1.0, member)
                share = jnp.where(hit, shares[k:k + 1, :], share)
            members.append(member)
            weights.append(share)
    earlier = (
        lax.broadcasted_iota(jnp.int32, (tokens, tokens), 0)
        < lax.broadcasted_iota(jnp.int32, (tokens, tokens), 1)
    )
    member = jnp.concatenate(members, axis=0)
    before = jnp.dot(
        member.astype(BF16), earlier.astype(F32).astype(BF16), preferred_element_type=F32
    )
    place_ref[...] = jnp.where(member > 0.0, before, -1.0).reshape(place_ref.shape)
    if share_ref is not None:
        share_ref[...] = jnp.concatenate(weights, axis=0).reshape(share_ref.shape)


def select_kernel(tiles, names_ref, *refs):
    blocks, metas = refs[:SIDE], refs[SIDE:2 * SIDE]
    outs, place_ref = refs[2 * SIDE:4 * SIDE], refs[4 * SIDE]
    capacity = outs[0].shape[2]
    experts = 2 * SIDE
    step = pl.program_id(0)

    @pl.when(step == 0)
    def _():
        settle(names_ref, metas, place_ref)

    tokens = metas[0].shape[2]
    slot = lax.broadcasted_iota(jnp.int32, (experts, capacity, tokens), 1).astype(F32)
    for i, j in [(i, j) for i in range(BATCH) for j in range(SIDE)]:
        block = blocks[j]
        place = place_ref[step * BATCH + i]
        pick = place[j * experts:(j + 1) * experts][:, None, :] == slot
        pick = pick.astype(F32).reshape(experts * capacity, tokens).astype(BF16)
        features = jnp.concatenate(
            [block[i, n * LANES:(n + 1) * LANES, :] for n in range(tiles)], axis=1
        )
        out = jnp.dot(pick, features, preferred_element_type=F32).astype(BF16)
        for p in range(SIDE):
            for e in range(2):
                row = (2 * p + e) * capacity
                outs[e * SIDE + p][i, j] = out[row:row + capacity, :]


def select(names, blocks, tiles, capacity):
    rows, width = blocks[0].shape[1], tiles * LANES
    at = width // META
    return pl.pallas_call(
        functools.partial(select_kernel, tiles),
        grid_spec=pltpu.PrefetchScalarGridSpec(
            num_scalar_prefetch=1,
            grid=(SIDE // BATCH,),
            in_specs=[pl.BlockSpec((BATCH, rows, LANES), lambda i, s: (i, 0, 0))] * SIDE
            + [pl.BlockSpec((SIDE, META, LANES), lambda i, s: (0, at, 0))] * SIDE,
            out_specs=[
                pl.BlockSpec((BATCH, SIDE, capacity, width), lambda i, s: (i, 0, 0, 0))
            ] * (2 * SIDE),
            scratch_shapes=[pltpu.VMEM((SIDE, 2 * SIDE * SIDE, LANES), F32)],
        ),
        out_shape=[jax.ShapeDtypeStruct((SIDE, SIDE, capacity, width), BF16)] * (2 * SIDE),
    )(names, *blocks, *blocks)


def combine_kernel(width, names_ref, *refs):
    metas, backs = refs[:SIDE], refs[SIDE:3 * SIDE]
    outs, place_ref, share_ref = refs[3 * SIDE:4 * SIDE], refs[4 * SIDE], refs[4 * SIDE + 1]
    capacity, full = backs[0].shape[2:]
    experts = 2 * SIDE
    slots = experts * capacity
    step = pl.program_id(0)

    @pl.when(step == 0)
    def _():
        settle(names_ref, metas, place_ref, share_ref)

    tokens = metas[0].shape[2]
    owner = lax.broadcasted_iota(jnp.int32, (experts, slots), 1) // capacity
    spread = (owner == lax.broadcasted_iota(jnp.int32, (experts, slots), 0))
    spread = spread.astype(F32).astype(BF16)
    slot = (lax.broadcasted_iota(jnp.int32, (tokens, slots), 1) % capacity).astype(F32)
    across = (((0,), (0,)), ((), ()))
    for i, j in [(i, j) for i in range(BATCH) for j in range(SIDE)]:
        here = slice(j * experts, (j + 1) * experts)
        place = place_ref[step * BATCH + i].astype(BF16)
        share = share_ref[step * BATCH + i].astype(BF16)
        taken = lax.dot_general(place[here], spread, across, preferred_element_type=F32)
        weight = lax.dot_general(share[here], spread, across, preferred_element_type=F32)
        pick = taken == slot
        weighted = jnp.where(pick, weight, 0.0).astype(BF16)
        back = jnp.concatenate(
            [backs[e * SIDE + p][i, j] for p in range(SIDE) for e in range(2)], axis=0
        )
        out = jnp.dot(weighted, back[:, :width], preferred_element_type=F32)
        outs[j][i, :, 0:width] = out.astype(BF16)
        if full > width:
            found = jnp.dot(
                pick.astype(F32).astype(BF16), back[:, width:], preferred_element_type=F32
            )
            outs[j][i, :, width:full] = found.astype(BF16)


def combine_slots(names, blocks, backs, tiles):
    capacity, full = backs[0].shape[2:]
    tokens = LANES
    at = tiles * LANES // META
    return pl.pallas_call(
        functools.partial(combine_kernel, tiles * LANES),
        grid_spec=pltpu.PrefetchScalarGridSpec(
            num_scalar_prefetch=1,
            grid=(SIDE // BATCH,),
            in_specs=[pl.BlockSpec((SIDE, META, LANES), lambda i, s: (0, at, 0))] * SIDE
            + [pl.BlockSpec((BATCH, SIDE, capacity, full), lambda i, s: (i, 0, 0, 0))] * (2 * SIDE),
            out_specs=[pl.BlockSpec((BATCH, tokens, full), lambda i, s: (i, 0, 0))] * SIDE,
            scratch_shapes=[pltpu.VMEM((SIDE, 2 * SIDE * SIDE, LANES), F32)] * 2,
        ),
        out_shape=[jax.ShapeDtypeStruct((SIDE, tokens, full), BF16)] * SIDE,
    )(names, *blocks, *backs)


def hidden_kernel(
    expert, table_ref, core_ref, *refs,
):
    wide, narrow = refs[:SIDE], refs[SIDE:2 * SIDE]
    down_mine, down_sent, out_ref, wide_v, narrow_v, down_v, sems = refs[2 * SIDE:]
    step = pl.program_id(0)
    groups, capacity, _ = wide_v.shape
    half = down_v.shape[0] // 2
    width = down_v.shape[1]
    batch = out_ref.shape[0] // capacity
    column = pl.multiple_of(core_ref[0] * width, LANES)
    copies = []
    per = groups // SIDE
    for p in range(SIDE):
        copies.append((wide[p], wide_v.at[p * per:(p + 1) * per]))
        copies.append((narrow[p], narrow_v.at[p * per:(p + 1) * per]))
    copies.append((down_mine.at[expert, :, pl.ds(column, width)], down_v.at[0:half]))
    copies.append((down_sent.at[expert, :, pl.ds(column, width)], down_v.at[half:2 * half]))
    copies = [
        pltpu.make_async_copy(a, b, sems.at[i]) for i, (a, b) in enumerate(copies)
    ]

    @pl.when(step == 0)
    def _():
        for copy in copies:
            copy.start()
        for copy in copies:
            copy.wait()

    first = step * batch
    rows = []
    for j in range(batch):
        rows.append(jnp.concatenate(
            [wide_v[table_ref[first + j]], narrow_v[table_ref[groups + first + j]]], axis=1
        ))
    out = lax.dot_general(
        jnp.concatenate(rows, axis=0), down_v[...], NT, preferred_element_type=F32
    )
    out_ref[...] = out.astype(BF16)


def hidden_step(expert, table, core, wide, narrow, down_mine, down_sent):
    groups = SIDE ** 3
    capacity, wide_width = wide[0].shape[1:]
    narrow_width = narrow[0].shape[2]
    width = wide_width + narrow_width
    hidden = 2 * down_mine.shape[1]
    batch = 256 // capacity
    hbm = pl.BlockSpec(memory_space=pl.ANY)
    return pl.pallas_call(
        functools.partial(hidden_kernel, expert),
        grid_spec=pltpu.PrefetchScalarGridSpec(
            num_scalar_prefetch=2,
            grid=(groups // batch,),
            in_specs=[hbm] * (2 * SIDE + 2),
            out_specs=pl.BlockSpec((batch * capacity, hidden), lambda i, *s: (i, 0)),
            scratch_shapes=[
                pltpu.VMEM((groups, capacity, wide_width), BF16),
                pltpu.VMEM((groups, capacity, narrow_width), BF16),
                pltpu.VMEM((hidden, width), BF16),
                pltpu.SemaphoreType.DMA((2 * SIDE + 2,)),
            ],
        ),
        out_shape=jax.ShapeDtypeStruct((groups * capacity, hidden), BF16),
        compiler_params=pltpu.CompilerParams(vmem_limit_bytes=56 * 1024 * 1024),
    )(table, core, *wide, *narrow, down_mine, down_sent)


def ready_kernel(gate_own, gate_other, up_own, up_other, *outs):
    for i, (gate_ref, up_ref) in enumerate(((gate_own, up_own), (gate_other, up_other))):
        gate = gate_ref[...].astype(F32)
        up = up_ref[...].astype(F32)
        s = jax.nn.sigmoid(gate)
        act = gate * s
        outs[3 * i][...] = act.astype(BF16)
        outs[3 * i + 1][...] = (up * (s * (1.0 + gate * (1.0 - s)))).astype(BF16)
        outs[3 * i + 2][...] = (act * up).astype(BF16)


def ready(saved):
    experts, rows, half = saved[0].shape
    batch = 256
    spec = pl.BlockSpec((1, batch, half), lambda e, i: (e, i, 0))
    return pl.pallas_call(
        ready_kernel,
        grid=(experts, rows // batch),
        in_specs=[spec] * 4,
        out_specs=[spec] * 6,
        out_shape=[jax.ShapeDtypeStruct(saved[0].shape, BF16)] * 6,
        name="ready",
    )(*saved)


def slot_kernel(
    expert, table_ref, core_ref, mine, sent,
    act_own, mix_own, both_own, act_other, mix_other, both_other,
    gatew_mine, gatew_sent, upw_mine, upw_sent, *refs,
):
    wide_out, narrow_out = refs[:SIDE], refs[SIDE:2 * SIDE]
    wide_v, narrow_v, mix_v, sems, out_sems = refs[2 * SIDE:]
    step = pl.program_id(0)
    groups, capacity, wide_full = wide_v.shape
    narrow_width = narrow_v.shape[2]
    width, quad = mix_v.shape
    wide_width = width - narrow_width
    half = quad // 4
    row = pl.multiple_of(core_ref[0] * width, LANES)
    copies = []
    for n, (a, b) in enumerate(((gatew_mine, gatew_sent), (upw_mine, upw_sent))):
        left = 2 * n * half
        copies.append(pltpu.make_async_copy(
            a.at[expert, pl.ds(row, width)], mix_v.at[:, left:left + half], sems.at[2 * n]))
        copies.append(pltpu.make_async_copy(
            b.at[expert, pl.ds(row, width)], mix_v.at[:, left + half:left + 2 * half], sems.at[2 * n + 1]))

    @pl.when(step == 0)
    def _():
        for copy in copies:
            copy.start()

    rows = mine.shape[0]
    batch = rows // capacity
    parts = []
    totals = []
    held = ((act_own, mix_own, both_own), (act_other, mix_other, both_other))
    for i, (act_ref, mix_ref, both_ref) in enumerate(held):
        a, b = i * half, (1 - i) * half
        g = mine[:, a:a + half].astype(F32) + sent[:, b:b + half].astype(F32)
        product = g * both_ref[0].astype(F32)
        parts.append((g * mix_ref[0].astype(F32)).astype(BF16))
        parts.append((g * act_ref[0].astype(F32)).astype(BF16))
        total = product[:, 0:LANES]
        for j in range(1, half // LANES):
            total = total + product[:, j * LANES:(j + 1) * LANES]
        totals.append(total)
    found = jnp.sum(totals[0] + totals[1], axis=1, keepdims=True)
    lane = lax.broadcasted_iota(jnp.int32, (rows, LANES), 1)
    found = jnp.where(lane == core_ref[1] + expert, found, 0.0).astype(BF16)

    @pl.when(step == 0)
    def _():
        for copy in copies:
            copy.wait()

    out = lax.dot_general(
        jnp.concatenate([parts[0], parts[2], parts[1], parts[3]], axis=1),
        mix_v[...], NT, preferred_element_type=F32,
    ).astype(BF16)
    for j in range(batch):
        here = slice(j * capacity, (j + 1) * capacity)
        at_wide = table_ref[step * batch + j]
        at_narrow = table_ref[groups + step * batch + j]
        wide_v[at_wide, :, 0:wide_width] = out[here, 0:wide_width]
        wide_v[at_wide, :, wide_width:wide_full] = found[here, :]
        narrow_v[at_narrow] = out[here, wide_width:width]

    @pl.when(step == pl.num_programs(0) - 1)
    def _():
        per = groups // SIDE
        leave = []
        for p in range(SIDE):
            leave.append(pltpu.make_async_copy(
                wide_v.at[p * per:(p + 1) * per], wide_out[p], out_sems.at[2 * p]))
            leave.append(pltpu.make_async_copy(
                narrow_v.at[p * per:(p + 1) * per], narrow_out[p], out_sems.at[2 * p + 1]))
        for copy in leave:
            copy.start()
        for copy in leave:
            copy.wait()


def slot_step(expert, table, core, mine, sent, saved, weights, capacity, wide_width, narrow_width):
    groups = SIDE ** 3
    rows, hidden = mine.shape
    half = hidden // 2
    batch = 256
    per = groups // SIDE
    hbm = pl.BlockSpec(memory_space=pl.ANY)
    block = pl.BlockSpec((batch, hidden), lambda i, *s: (i, 0))
    kept = pl.BlockSpec((1, batch, half), lambda i, *s: (expert, i, 0))
    wide_full = wide_width + LANES
    width = wide_width + narrow_width
    return pl.pallas_call(
        functools.partial(slot_kernel, expert),
        grid_spec=pltpu.PrefetchScalarGridSpec(
            num_scalar_prefetch=2,
            grid=(rows // batch,),
            in_specs=[block, block] + [kept] * 6 + [hbm] * 4,
            out_specs=[hbm] * (2 * SIDE),
            scratch_shapes=[
                pltpu.VMEM((groups, capacity, wide_full), BF16),
                pltpu.VMEM((groups, capacity, narrow_width), BF16),
                pltpu.VMEM((width, 4 * half), BF16),
                pltpu.SemaphoreType.DMA((4,)),
                pltpu.SemaphoreType.DMA((2 * SIDE,)),
            ],
        ),
        out_shape=[jax.ShapeDtypeStruct((per, capacity, wide_full), BF16)] * SIDE
        + [jax.ShapeDtypeStruct((per, capacity, narrow_width), BF16)] * SIDE,
        compiler_params=pltpu.CompilerParams(vmem_limit_bytes=56 * 1024 * 1024),
    )(table, core, mine, sent, *saved, *weights)


def total_of(parts):
    total = parts[0].astype(F32)
    for part in parts[1:]:
        total = total + part.astype(F32)
    return total


def finish_kernel(ids_ref, *refs):
    wide, narrow = refs[:SIDE], refs[SIDE:2 * SIDE]
    tokens_ref, grad_combine_ref = refs[2 * SIDE:]
    tokens = tokens_ref.shape[0]
    wide_width = wide[0].shape[1] - LANES
    total = total_of([ref[...] for ref in wide])
    tokens_ref[:, 0:wide_width] = total[:, 0:wide_width].astype(BF16)
    tokens_ref[:, wide_width:] = total_of([ref[...] for ref in narrow]).astype(BF16)
    found = total[:, wide_width:].T
    names = lax.broadcasted_iota(jnp.int32, (LANES, tokens), 0)
    rows = [
        jnp.sum(jnp.where(ids_ref[k:k + 1, :] == names, found, 0.0), axis=0, keepdims=True)
        for k in range(TOP)
    ]
    grad_combine_ref[...] = jnp.concatenate(rows, axis=0).astype(BF16)


def finish(ids, wide, narrow):
    tokens = wide[0].shape[0]
    width = wide[0].shape[1] - LANES + narrow[0].shape[1]
    return pl.pallas_call(
        finish_kernel,
        out_shape=[
            jax.ShapeDtypeStruct((tokens, width), BF16),
            jax.ShapeDtypeStruct((TOP, tokens), BF16),
        ],
        name="finish",
    )(ids, *wide, *narrow)


def on_device(
    grad_out, combine, expert_ids, saved_gate, saved_up, gate_weight, up_weight, down_weight
):
    groups = lax.axis_size("expert")
    core = lax.axis_index("etp")
    chip = lax.axis_index("expert")
    width = grad_out.shape[1]
    capacity = saved_gate.shape[0] // groups
    ids, shares = expert_ids.T, combine.T
    tiles = (9, width // LANES - 9)
    lanes = (WIDE, NARROW)

    me = jnp.stack(coords(chip))
    order = jnp.stack(coords(jnp.arange(groups, dtype=jnp.int32)))
    apart = (order - me[:, None]) % SIDE
    tables, names = [], []
    for lane in lanes:
        axes = jnp.where(core == 0, jnp.array(lane[0]), jnp.array(lane[1]))
        step = jnp.take(apart, axes, axis=0)
        tables.append(step[2] * SIDE * SIDE + step[0] * SIDE + step[1])
        along = jnp.arange(SIDE, dtype=jnp.int32)[None, :] * (
            jnp.arange(3)[:, None] == axes[2]
        )
        column = joined((me[:, None] + along) % SIDE)
        names.append((column[:, None] * 2 + jnp.arange(2)[None, :]).reshape(-1).astype(jnp.int32))
    table = jnp.concatenate(tables).astype(jnp.int32)
    place = jnp.stack([core, chip * 2]).astype(jnp.int32)

    blocks = prepare(grad_out, ids, shares, tiles)
    stage = []
    for n, lane in enumerate(lanes):
        parts = gathered(blocks[n], lane, 0)
        stage.append(jnp.stack(parts))
    stage = [gathered(b, lane, 1) for b, lane in zip(stage, lanes)]
    arrived = [[], []]
    for n, lane in enumerate(lanes):
        slots = select(names[n], stage[n], tiles[n], capacity)
        for e in range(2):
            got = scattered(slots[e * SIDE:(e + 1) * SIDE], lane, 2)
            arrived[e].append([x.reshape(SIDE * SIDE, capacity, x.shape[-1]) for x in got])

    swap = [(0, 1), (1, 0)]

    def swapped(x):
        return lax.ppermute(x, "etp", swap)

    saved = []
    for x in (saved_gate, saved_up):
        own = x.transpose(1, 0, 2)
        saved += [own, swapped(own)]
    down_sent, gate_sent, up_sent = [swapped(x) for x in (down_weight, gate_weight, up_weight)]
    saved = ready(saved)

    mine, sent = [], []
    for e in range(2):
        mine.append(
            hidden_step(e, table, place, arrived[e][0], arrived[e][1], down_weight, down_sent)
        )
        sent.append(swapped(mine[e]))
    returned = [[], []]
    for e in range(2):
        pieces = slot_step(
            e, table, place, mine[e], sent[e], saved,
            (gate_weight, gate_sent, up_weight, up_sent),
            capacity, tiles[0] * LANES, tiles[1] * LANES,
        )
        for n, lane in enumerate(lanes):
            backs = [
                x.reshape(SIDE, SIDE, capacity, x.shape[-1])
                for x in pieces[n * SIDE:(n + 1) * SIDE]
            ]
            returned[n] += scattered(backs, lane, 2)
    ends = []
    for n, lane in enumerate(lanes):
        backs = returned[n]
        backs = combine_slots(names[n], stage[n], backs, tiles[n])
        backs = scattered(backs, lane, 1)
        total = [total_of([b[i] for b in backs]).astype(BF16) for i in range(SIDE)]
        ends.append(scattered(total, lane, 0))
    grad_tokens, grad_combine = finish(ids, ends[0], ends[1])
    return grad_tokens, grad_combine.T


def solution(mesh):
    in_specs = (
        P("expert", "etp"),
        P("expert", None),
        P("expert", None),
        P(None, "expert", "etp"),
        P(None, "expert", "etp"),
        P("expert", None, "etp"),
        P("expert", None, "etp"),
        P("expert", "etp", None),
    )
    out_specs = (P("expert", "etp"), P("expert", None))

    return jax.shard_map(
        on_device, mesh=mesh, in_specs=in_specs, out_specs=out_specs, check_vma=False
    )
```

time: 434 us -> 364 us (0.84)
  local copies, waits for them, and re-layouts: 119 us -> 13.2 us
  blocking collectives: 99.3 us -> 0 us
  Pallas kernels: 0 us -> 94.1 us
  starting transfers between devices: 27.6 us -> 87.8 us
  matrix products: 54.9 us -> 0 us
  waiting for transfers between devices: 105 us -> 156 us
  between operations: 14.2 us -> 1.18 us
    ppermute x0 -> x55, waiting for transfers between devices: none -> 156 us  [the longest x48 156 us: moved(): return lax.ppermute(x, BOTH, pairs)]
    all_to_all x2 -> x0, blocking collectives: 99.3 us -> none  [the longest x1 95.6 us: on_device(): lax.all_to_all(outgoing, 'expert', split_axis=0, concat_axis=0, tiled=True)]
    pallas_call x0 -> x11, Pallas kernels: none -> 94.1 us  [the longest x2 35.4 us: slot_step(): pl.pallas_call(functools.partial(slot_kernel, expert), grid_spec=pltpu.Pr...]
    all_to_all x3 -> x0, waiting for transfers between devices: 94.1 us -> none  [the longest x1 94.1 us: on_device(): lax.all_to_all(slot_grad, 'expert', split_axis=0, concat_axis=0, tiled=True)]
    ppermute x0 -> x55, starting transfers between devices: none -> 87.8 us  [the longest x48 86.6 us: moved(): return lax.ppermute(x, BOTH, pairs)]
    gather x6 -> x2, local copies, waits for them, and re-layouts: 57.6 us -> 1.11 us  [on_device(): step = jnp.take(apart, axes, axis=0)]
    dot_general x3 -> x0, matrix products: 54.9 us -> none  [the longest x1 20.6 us: on_device(): jnp.einsum('rlf,ldf->rld', grad_up, up_weight, preferred_element_type=jnp...]
    all_to_all x3 -> x0, starting transfers between devices: 27.3 us -> none  [the longest x1 10.5 us: on_device(): lax.all_to_all(slot_grad, 'expert', split_axis=0, concat_axis=0, tiled=True)]
  transfers between devices with their start and end apart: 5 -> 55, of which waited for: 2 -> 24; matrix products, arithmetic and copies ran while one was open for 10% -> 4% of each run, Pallas kernels for 0% -> 25%
where the time goes in v2:
time: 364 us; the launch traced here: 360 us
  waiting for transfers between devices  156 us (43%)
  Pallas kernels  94.1 us (26%)
  starting transfers between devices  87.8 us (24%)
  local copies, waits for them, and re-layouts  13.2 us (4%)
  other arithmetic  8.22 us (2%)
    ppermute x48, waiting for transfers between devices, moved(): return lax.ppermute(x, BOTH, pairs)  156 us
    ppermute x48, starting transfers between devices, moved(): return lax.ppermute(x, BOTH, pairs)  86.6 us
    pallas_call x2, Pallas kernels, slot_step(): pl.pallas_call(functools.partial(slot_kernel, expert), grid_spec=pltpu.Pr...  35.4 us
    pallas_call x2, Pallas kernels, hidden_step(): pl.pallas_call(functools.partial(hidden_kernel, expert), grid_spec=pltpu....  19 us
    pallas_call x2, Pallas kernels, combine_slots(): pl.pallas_call(functools.partial(combine_kernel, tiles * LANES), grid_spe...  14.6 us
    pallas_call x1, Pallas kernels, ready(): pl.pallas_call(ready_kernel, grid=(experts, rows // batch), in_specs=[spe...  10.8 us
    unnamed x82, local copies, waits for them, and re-layouts  10.2 us
    pallas_call x2, Pallas kernels, select(): pl.pallas_call(functools.partial(select_kernel, tiles), grid_spec=pltpu.P...  9.86 us
  transfers between devices with their start and end apart: 55, of which 24 were waited for; matrix products, arithmetic and copies ran while one was open for 4% of the time, Pallas kernels for 25%

profile of v2, /device:TPU:34, one launch (start us, length us, event | category | flops | bytes accessed | tf_op | source)
XLA Modules:
  0.0 360.4 jit_solution(14303508977364522931)
XLA Ops:
  24.8 14.6 %collective-permute-done = bf16[1168,128]{1,0:T(8,128)(2,1)S(1)} collective-permute-done((bf16[1168,128]{1,0:T(8,128)(2,1)}, bf16[1168,128]{1,0:T(8,128)(2,1)S(1)}, u32[]{:S(2)}, u32[]{:S(2)}) %collective-permute-start) | collective-permute-done | bytes 299040 | tf_op jit(solution)/shard_map/ppermute | solution.py:41
  42.9 7.5 %collective-permute-done.13.refs_2_.refs_6_ = bf16[4,656,128]{2,1,0:T(8,128)(2,1)} collective-permute-done((bf16[4,656,128]{2,1,0:T(8,128)(2,1)S(1)}, bf16[4,656,128]{2,1,0:T(8,128)(2,1)}, u32[]{:S(2)}, u32[]{:S(2)}) %collective-permute-start.13) | collective-permute-done | bytes 671776 | tf_op jit(solution)/shard_map/ppermute | solution.py:41
  53.6 4.2 %shard_map.132 = (bf16[4,4,16,640]{3,2,1,0:T(8,128)(2,1)}, bf16[4,4,16,640]{3,2,1,0:T(8,128)(2,1)}, bf16[4,4,16,640]{3,2,1,0:T(8,128)(2,1)}, bf16[4,4,16,640]{3,...) custom-call(s32[8]{0:T(128)} %add.313.names_ref, ...), custom_call_target="tpu_custom_call" | custom-call | tf_op jit(solution)/shard_map/pallas_call | solution.py:138
  59.0 6.6 %collective-permute-done.15 = bf16[4,4,16,640]{3,2,1,0:T(8,128)(2,1)S(1)} collective-permute-done((bf16[4,4,16,640]{3,2,1,0:T(8,128)(2,1)}, bf16[4,4,16,640]{3,2,1,0:T(8,128)(2,1)S(1)}, u32[]{:S(2)}, u32[]{:S(2)}) %collective-permute-start.15) | collective-permute-done | bytes 327712 | tf_op jit(solution)/shard_map/ppermute | solution.py:41
  65.6 6.5 %collective-permute-start.16 = (bf16[4,4,16,640]{3,2,1,0:T(8,128)(2,1)}, bf16[4,4,16,640]{3,2,1,0:T(8,128)(2,1)S(1)}, u32[]{:S(2)}, u32[]{:S(2)}) collective-permute-start(bf16[4,4,16,640]{3,2,1,0:T(8,128)(2,1)} %get-tuple-element.61), channel_id=1, source_target_pairs={{0,16},{1,17},{2,18},{3,19},{4,20},{5,21},{6,22},{7,23},{8,24},{9,... | collective-permute-start | bytes 983048 | tf_op jit(solution)/shard_map/ppermute | solution.py:41
  72.1 5.3 %collective-permute-done.16 = bf16[4,4,16,640]{3,2,1,0:T(8,128)(2,1)S(1)} collective-permute-done((bf16[4,4,16,640]{3,2,1,0:T(8,128)(2,1)}, bf16[4,4,16,640]{3,2,1,0:T(8,128)(2,1)S(1)}, u32[]{:S(2)}, u32[]{:S(2)}) %collective-permute-start.16) | collective-permute-done | bytes 327712 | tf_op jit(solution)/shard_map/ppermute | solution.py:41
  79.8 7.5 %collective-permute-done.17 = bf16[4,4,16,640]{3,2,1,0:T(8,128)(2,1)} collective-permute-done((bf16[4,4,16,640]{3,2,1,0:T(8,128)(2,1)}, bf16[4,4,16,640]{3,2,1,0:T(8,128)(2,1)}, u32[]{:S(2)}, u32[]{:S(2)}) %collective-permute-start.17) | collective-permute-done | bytes 327712 | tf_op jit(solution)/shard_map/ppermute | solution.py:41
  90.7 18.1 %collective-permute-done.4.refs_2_.refs_6_ = bf16[4,1168,128]{2,1,0:T(8,128)(2,1)S(1)} collective-permute-done((bf16[4,1168,128]{2,1,0:T(8,128)(2,1)S(1)}, bf16[4,1168,128]{2,1,0:T(8,128)(2,1)S(1)}, u32[]{:S(2)}, u32[]{:S(2)}) %collective-permute-start.4) | collective-permute-done | bytes 1196064 | tf_op jit(solution)/shard_map/ppermute | solution.py:41
  108.8 16.3 %collective-permute-done.3.refs_1_.refs_5_ = bf16[4,1168,128]{2,1,0:T(8,128)(2,1)S(1)} collective-permute-done((bf16[4,1168,128]{2,1,0:T(8,128)(2,1)S(1)}, bf16[4,1168,128]{2,1,0:T(8,128)(2,1)S(1)}, u32[]{:S(2)}, u32[]{:S(2)}) %collective-permute-start.3) | collective-permute-done | bytes 1196064 | tf_op jit(solution)/shard_map/ppermute | solution.py:41
  128.4 5.6 %shard_map.131 = (bf16[4,4,16,1152]{3,2,1,0:T(8,128)(2,1)}, bf16[4,4,16,1152]{3,2,1,0:T(8,128)(2,1)}, bf16[4,4,16,1152]{3,2,1,0:T(8,128)(2,1)}, bf16[4,4,16,1152...) custom-call(s32[8]{0:T(128)} %add.295.names_ref, ...), custom_call_target="tpu_custom_call" | custom-call | tf_op jit(solution)/shard_map/pallas_call | solution.py:138
  135.5 6.5 %collective-permute-done.32 = bf16[4,4,16,640]{3,2,1,0:T(8,128)(2,1)S(1)} collective-permute-done((bf16[4,4,16,640]{3,2,1,0:T(8,128)(2,1)S(1)}, bf16[4,4,16,640]{3,2,1,0:T(8,128)(2,1)S(1)}, u32[]{:S(2)}, u32[]{:S(2)}) %collective-permute-start.32) | collective-permute-done | bytes 327712 | tf_op jit(solution)/shard_map/ppermute | solution.py:41
  146.6 6.9 %collective-permute-done.7 = bf16[4,4,16,1152]{3,2,1,0:T(8,128)(2,1)S(1)} collective-permute-done((bf16[4,4,16,1152]{3,2,1,0:T(8,128)(2,1)}, bf16[4,4,16,1152]{3,2,1,0:T(8,128)(2,1)S(1)}, u32[]{:S(2)}, u32[]{:S(2)}) %collective-permute-start.7) | collective-permute-done | bytes 589856 | tf_op jit(solution)/shard_map/ppermute | solution.py:41
  157.0 3.5 collective-permute-done.8
  160.5 4.0 %collective-permute-done.27 = bf16[4,4,16,1152]{3,2,1,0:T(8,128)(2,1)S(1)} collective-permute-done((bf16[4,4,16,1152]{3,2,1,0:T(8,128)(2,1)}, bf16[4,4,16,1152]{3,2,1,0:T(8,128)(2,1)S(1)}, u32[]{:S(2)}, u32[]{:S(2)}) %collective-permute-start.27) | collective-permute-done | bytes 589856 | tf_op jit(solution)/shard_map/ppermute | solution.py:41
  164.5 4.4 %collective-permute-start.28 = (bf16[4,4,16,1152]{3,2,1,0:T(8,128)(2,1)}, bf16[4,4,16,1152]{3,2,1,0:T(8,128)(2,1)S(1)}, u32[]{:S(2)}, u32[]{:S(2)}) collective-permute-start(bf16[4,4,16,1152]{3,2,1,0:T(8,128)(2,1)} %get-tuple-element.75), channel_id=1, source_target_pairs={{0,4},{1,65},{2,6},{3,67},{4,0},{5,69},{6,2},{7,71},{8,12},{9,73},... | collective-permute-start | bytes 1769480 | tf_op jit(solution)/shard_map/ppermute | solution.py:41
  169.6 7.3 %collective-permute-done.28 = bf16[4,4,16,1152]{3,2,1,0:T(8,128)(2,1)S(1)} collective-permute-done((bf16[4,4,16,1152]{3,2,1,0:T(8,128)(2,1)}, bf16[4,4,16,1152]{3,2,1,0:T(8,128)(2,1)S(1)}, u32[]{:S(2)}, u32[]{:S(2)}) %collective-permute-start.28) | collective-permute-done | bytes 589856 | tf_op jit(solution)/shard_map/ppermute | solution.py:41
  182.1 9.5 %shard_map.133.mine = bf16[1024,1024]{1,0:T(8,128)(2,1)} custom-call(s32[128]{0:T(128)} %pad_add_fusion.1.table_ref, s32[2]{0:T(128)} %pad_add_fusion.2.core_ref, bf16[16,16,1152]{2,1,0:T(8,128)(2,1)} %bitcast.86, bf16[16,16,1152]{2,1,0:T(8,128)(2,1)} %bitcast.87, bf16[16,16,1152]{2,1,0:T(8,128)(2,1)} %bitcast.89, bf16[16,16,1152]{2,1,0:T(8,128)(2,1)} %bitcast.90, ...), custom_call_target="tpu_custom_call" | custom-call | tf_op jit(solution)/shard_map/pallas_call | solution.py:259
  192.2 9.5 %shard_map.135.mine = bf16[1024,1024]{1,0:T(8,128)(2,1)} custom-call(s32[128]{0:T(128)} %pad_add_fusion.1.table_ref, s32[2]{0:T(128)} %pad_add_fusion.2.core_ref, bf16[16,16,1152]{2,1,0:T(8,128)(2,1)} %bitcast.85, bf16[16,16,1152]{2,1,0:T(8,128)(2,1)} %bitcast.88, bf16[16,16,1152]{2,1,0:T(8,128)(2,1)} %bitcast.91, bf16[16,16,1152]{2,1,0:T(8,128)(2,1)} %bitcast.37.refs_3_, ...), custom_call_target="tpu_custom_call" | custom-call | tf_op jit(solution)/shard_map/pallas_call | solution.py:259
  201.9 10.8 %ready.1 = (bf16[2,1024,512]{2,1,0:T(8,128)(2,1)}, bf16[2,1024,512]{2,1,0:T(8,128)(2,1)}, bf16[2,1024,512]{2,1,0:T(8,128)(2,1)}, bf16[2,1024,512]{2,1,0:T(8,128)...) custom-call(bf16[2,1024,512]{2,1,0:T(8,128)(2,1)} %bitcast.82, ...), custom_call_target="tpu_custom_call" | custom-call | tf_op jit(solution)/shard_map/ready/pallas_call | solution.py:293
  212.7 17.7 %shard_map.134 = (bf16[16,16,1280]{2,1,0:T(8,128)(2,1)}, bf16[16,16,1280]{2,1,0:T(8,128)(2,1)}, bf16[16,16,1280]{2,1,0:T(8,128)(2,1)}, bf16[16,16,1280]{2,1,0:T(...) custom-call(s32[128]{0:T(128)} %pad_add_fusion.1.table_ref, ...), custom_call_target="tpu_custom_call" | custom-call | tf_op jit(solution)/shard_map/pallas_call | solution.py:392
  237.1 17.7 %shard_map.136 = (bf16[16,16,1280]{2,1,0:T(8,128)(2,1)}, bf16[16,16,1280]{2,1,0:T(8,128)(2,1)}, bf16[16,16,1280]{2,1,0:T(8,128)(2,1)}, bf16[16,16,1280]{2,1,0:T(...) custom-call(s32[128]{0:T(128)} %pad_add_fusion.1.table_ref, ...), custom_call_target="tpu_custom_call" | custom-call | tf_op jit(solution)/shard_map/pallas_call | solution.py:392
  254.9 3.3 collective-permute-start.47
  259.1 3.5 collective-permute-start.25
  267.3 4.4 %collective-permute-done.47.refs_10_ = bf16[4,4,16,640]{3,2,1,0:T(8,128)(2,1)S(1)} collective-permute-done((bf16[4,4,16,640]{3,2,1,0:T(8,128)(2,1)}, bf16[4,4,16,640]{3,2,1,0:T(8,128)(2,1)S(1)}, u32[]{:S(2)}, u32[]{:S(2)}) %collective-permute-start.47) | collective-permute-done | bytes 327712 | tf_op jit(solution)/shard_map/ppermute | solution.py:41
  273.3 3.5 collective-permute-start.35
  277.7 6.6 %shard_map.138 = (bf16[4,128,640]{2,1,0:T(8,128)(2,1)}, bf16[4,128,640]{2,1,0:T(8,128)(2,1)}, bf16[4,128,640]{2,1,0:T(8,128)(2,1)}, bf16[4,128,640]{2,1,0:T(8,128)(2,1)}) custom-call(s32[8]{0:T(128)} %add.313.names_ref, bf16[4,656,128]{2,1,0:T(8,128)(2,1)} %copy-done.4, bf16[4,656,128]{2,1,0:T(8,128)(2,1)} %collective-permute-done.12.refs_1_.refs_5_, ...), custom_call_target="tpu_custom_call" | custom-call | tf_op jit(solution)/shard_map/pallas_call | solution.py:196
  286.8 5.8 %collective-permute-done.35.refs_10_ = bf16[4,4,16,1280]{3,2,1,0:T(8,128)(2,1)S(1)} collective-permute-done((bf16[4,4,16,1280]{3,2,1,0:T(8,128)(2,1)}, bf16[4,4,16,1280]{3,2,1,0:T(8,128)(2,1)S(1)}, u32[]{:S(2)}, u32[]{:S(2)}) %collective-permute-start.35) | collective-permute-done | bytes 655392 | tf_op jit(solution)/shard_map/ppermute | solution.py:41
  293.7 8.0 %shard_map.137 = (bf16[4,128,1280]{2,1,0:T(8,128)(2,1)}, bf16[4,128,1280]{2,1,0:T(8,128)(2,1)}, bf16[4,128,1280]{2,1,0:T(8,128)(2,1)}, bf16[4,128,1280]{2,1,0:T(8,128)(2,1)}) custom-call(s32[8]{0:T(128)} %add.295.names_ref, bf16[4,1168,128]{2,1,0:T(8,128)(2,1)} %copy-done, bf16[4,1168,128]{2,1,0:T(8,128)(2,1)} %copy-done.3, bf16[4,1168,128]{2,1,0:T(8,128)(2,1)} %copy-done.2, ...), custom_call_target="tpu_custom_call" | custom-call | tf_op jit(solution)/shard_map/pallas_call | solution.py:196
  301.7 3.4 collective-permute-start.37
  312.3 17.2 %collective-permute-done.50 = bf16[4,128,640]{2,1,0:T(8,128)(2,1)S(1)} collective-permute-done((bf16[4,128,640]{2,1,0:T(8,128)(2,1)}, bf16[4,128,640]{2,1,0:T(8,128)(2,1)S(1)}, u32[]{:S(2)}, u32[]{:S(2)}) %collective-permute-start.50) | collective-permute-done | bytes 655392 | tf_op jit(solution)/shard_map/ppermute | solution.py:41
  329.5 7.5 %collective-permute-done.51 = bf16[4,128,640]{2,1,0:T(8,128)(2,1)S(1)} collective-permute-done((bf16[4,128,640]{2,1,0:T(8,128)(2,1)}, bf16[4,128,640]{2,1,0:T(8,128)(2,1)S(1)}, u32[]{:S(2)}, u32[]{:S(2)}) %collective-permute-start.51) | collective-permute-done | bytes 655392 | tf_op jit(solution)/shard_map/ppermute | solution.py:41
  352.0 4.7 %collective-permute-done.52.refs_5_ = bf16[128,640]{1,0:T(8,128)(2,1)S(1)} collective-permute-done((bf16[128,640]{1,0:T(8,128)(2,1)S(1)}, bf16[128,640]{1,0:T(8,128)(2,1)S(1)}, u32[]{:S(2)}, u32[]{:S(2)}) %collective-permute-start.52) | collective-permute-done | bytes 163872 | tf_op jit(solution)/shard_map/ppermute | solution.py:41
  (199 shorter events, 101.2 us)
Async XLA Ops:
  0.6 181.5 %collective-permute-start.18 = (bf16[2,512,3584]{2,1,0:T(8,128)(2,1)}, bf16[2,512,3584]{2,1,0:T(8,128)(2,1)}, u32[]{:S(2)}, u32[]{:S(2)}) collective-permute-start(bf16[2,512,3584]{2,1,0:T(8,128)(2,1)} %refs_8_.3), channel_id=1, source_target_pairs={{0,1},{1,0},{2,3},{3,2},{4,5},{5,4},{6,7},{7,6},{8,9},{9,8},{10,11... | collective-permute-start | bytes 22020104 | tf_op jit(solution)/shard_map/ppermute | solution.py:494
  16.0 23.4 %collective-permute-start = (bf16[1168,128]{1,0:T(8,128)(2,1)}, bf16[1168,128]{1,0:T(8,128)(2,1)S(1)}, u32[]{:S(2)}, u32[]{:S(2)}) collective-permute-start(bf16[1168,128]{1,0:T(8,128)(2,1)} %get-tuple-element.53), channel_id=1, source_target_pairs={{0,96},{1,25},{2,98},{3,27},{4,100},{5,29},{6,102},{7,31},{8,104},... | collective-permute-start | bytes 897032 | tf_op jit(solution)/shard_map/ppermute | solution.py:41
  18.1 24.8 %collective-permute-start.14 = (bf16[4,656,128]{2,1,0:T(8,128)(2,1)S(1)}, bf16[4,656,128]{2,1,0:T(8,128)(2,1)}, u32[]{:S(2)}, u32[]{:S(2)}) collective-permute-start(bf16[4,656,128]{2,1,0:T(8,128)(2,1)S(1)} %pad_maximum_fusion.1.refs_0_.refs_4_), channel_id=1, source_target_pairs={{0,32},{1,33},{2,34},{3,35},{4,36},{5,37},{6,38},{7,39},{8,40},{9,... | collective-permute-start | bytes 2015240 | tf_op jit(solution)/shard_map/ppermute | solution.py:41
  19.1 31.3 %collective-permute-start.13 = (bf16[4,656,128]{2,1,0:T(8,128)(2,1)S(1)}, bf16[4,656,128]{2,1,0:T(8,128)(2,1)}, u32[]{:S(2)}, u32[]{:S(2)}) collective-permute-start(bf16[4,656,128]{2,1,0:T(8,128)(2,1)S(1)} %pad_maximum_fusion.1.refs_0_.refs_4_), channel_id=1, source_target_pairs={{0,64},{1,65},{2,66},{3,67},{4,68},{5,69},{6,70},{7,71},{8,72},{9,... | collective-permute-start | bytes 2015240 | tf_op jit(solution)/shard_map/ppermute | solution.py:41
  22.7 31.0 %collective-permute-start.12 = (bf16[4,656,128]{2,1,0:T(8,128)(2,1)S(1)}, bf16[4,656,128]{2,1,0:T(8,128)(2,1)}, u32[]{:S(2)}, u32[]{:S(2)}) collective-permute-start(bf16[4,656,128]{2,1,0:T(8,128)(2,1)S(1)} %pad_maximum_fusion.1.refs_0_.refs_4_), channel_id=1, source_target_pairs={{0,96},{1,97},{2,98},{3,99},{4,100},{5,101},{6,102},{7,103},{8,104... | collective-permute-start | bytes 2015240 | tf_op jit(solution)/shard_map/ppermute | solution.py:41
  40.5 48.5 %collective-permute-start.5 = (bf16[4,1168,128]{2,1,0:T(8,128)(2,1)S(1)}, bf16[4,1168,128]{2,1,0:T(8,128)(2,1)S(1)}, u32[]{:S(2)}, u32[]{:S(2)}) collective-permute-start(bf16[4,1168,128]{2,1,0:T(8,128)(2,1)S(1)} %pad_maximum_fusion.refs_0_.refs_4_), channel_id=1, source_target_pairs={{0,8},{1,3},{2,10},{3,5},{4,12},{5,7},{6,14},{7,1},{8,16},{9,11},{... | collective-permute-start | bytes 3588104 | tf_op jit(solution)/shard_map/ppermute | solution.py:41
  58.5 154.1 %collective-permute-start.22 = (bf16[2,3584,512]{2,1,0:T(8,128)(2,1)}, bf16[2,3584,512]{2,1,0:T(8,128)(2,1)}, u32[]{:S(2)}, u32[]{:S(2)}) collective-permute-start(bf16[2,3584,512]{2,1,0:T(8,128)(2,1)} %gatew_mine.3), channel_id=1, source_target_pairs={{0,1},{1,0},{2,3},{3,2},{4,5},{5,4},{6,7},{7,6},{8,9},{9,8},{10,11... | collective-permute-start | bytes 22020104 | tf_op jit(solution)/shard_map/ppermute | solution.py:494
  58.5 154.2 %collective-permute-start.23 = (bf16[2,3584,512]{2,1,0:T(8,128)(2,1)}, bf16[2,3584,512]{2,1,0:T(8,128)(2,1)}, u32[]{:S(2)}, u32[]{:S(2)}) collective-permute-start(bf16[2,3584,512]{2,1,0:T(8,128)(2,1)} %upw_mine.3), channel_id=1, source_target_pairs={{0,1},{1,0},{2,3},{3,2},{4,5},{5,4},{6,7},{7,6},{8,9},{9,8},{10,11... | collective-permute-start | bytes 22020104 | tf_op jit(solution)/shard_map/ppermute | solution.py:494
  87.4 21.4 %collective-permute-start.4 = (bf16[4,1168,128]{2,1,0:T(8,128)(2,1)S(1)}, bf16[4,1168,128]{2,1,0:T(8,128)(2,1)S(1)}, u32[]{:S(2)}, u32[]{:S(2)}) collective-permute-start(bf16[4,1168,128]{2,1,0:T(8,128)(2,1)S(1)} %pad_maximum_fusion.refs_0_.refs_4_), channel_id=1, source_target_pairs={{0,16},{1,5},{2,18},{3,7},{4,20},{5,1},{6,22},{7,3},{8,24},{9,13},... | collective-permute-start | bytes 3588104 | tf_op jit(solution)/shard_map/ppermute | solution.py:41
  89.0 36.1 %collective-permute-start.3 = (bf16[4,1168,128]{2,1,0:T(8,128)(2,1)S(1)}, bf16[4,1168,128]{2,1,0:T(8,128)(2,1)S(1)}, u32[]{:S(2)}, u32[]{:S(2)}) collective-permute-start(bf16[4,1168,128]{2,1,0:T(8,128)(2,1)S(1)} %pad_maximum_fusion.refs_0_.refs_4_), channel_id=1, source_target_pairs={{0,24},{1,7},{2,26},{3,1},{4,28},{5,3},{6,30},{7,5},{8,0},{9,15},{... | collective-permute-start | bytes 3588104 | tf_op jit(solution)/shard_map/ppermute | solution.py:41
  108.8 25.2 %collective-permute-start.30 = (bf16[4,4,16,640]{3,2,1,0:T(8,128)(2,1)}, bf16[4,4,16,640]{3,2,1,0:T(8,128)(2,1)S(1)}, u32[]{:S(2)}, u32[]{:S(2)}) collective-permute-start(bf16[4,4,16,640]{3,2,1,0:T(8,128)(2,1)} %get-tuple-element.78), channel_id=1, source_target_pairs={{0,24},{1,25},{2,26},{3,27},{4,28},{5,29},{6,30},{7,31},{8,0},{9,1... | collective-permute-start | bytes 983048 | tf_op jit(solution)/shard_map/ppermute | solution.py:41
  160.4 41.3 %collective-permute-start.21 = (bf16[2,1024,512]{2,1,0:T(8,128)(2,1)S(1)}, bf16[2,1024,512]{2,1,0:T(8,128)(2,1)}, u32[]{:S(2)}, u32[]{:S(2)}) collective-permute-start(bf16[2,1024,512]{2,1,0:T(8,128)(2,1)S(1)} %bitcast.79), channel_id=1, source_target_pairs={{0,1},{1,0},{2,3},{3,2},{4,5},{5,4},{6,7},{7,6},{8,9},{9,8},{10,11... | collective-permute-start | bytes 6291464 | tf_op jit(solution)/shard_map/ppermute | solution.py:494
  182.1 19.7 %collective-permute-start.20 = (bf16[2,1024,512]{2,1,0:T(8,128)(2,1)S(1)}, bf16[2,1024,512]{2,1,0:T(8,128)(2,1)}, u32[]{:S(2)}, u32[]{:S(2)}) collective-permute-start(bf16[2,1024,512]{2,1,0:T(8,128)(2,1)S(1)} %bitcast.81), channel_id=1, source_target_pairs={{0,1},{1,0},{2,3},{3,2},{4,5},{5,4},{6,7},{7,6},{8,9},{9,8},{10,11... | collective-permute-start | bytes 6291464 | tf_op jit(solution)/shard_map/ppermute | solution.py:494
  191.7 21.0 %collective-permute-start.19 = (bf16[1024,1024]{1,0:T(8,128)(2,1)}, bf16[1024,1024]{1,0:T(8,128)(2,1)}, u32[]{:S(2)}, u32[]{:S(2)}) collective-permute-start(bf16[1024,1024]{1,0:T(8,128)(2,1)} %shard_map.133.mine), channel_id=1, source_target_pairs={{0,1},{1,0},{2,3},{3,2},{4,5},{5,4},{6,7},{7,6},{8,9},{9,8},{10,11... | collective-permute-start | bytes 6291464 | tf_op jit(solution)/shard_map/ppermute | solution.py:494
  201.8 34.0 %collective-permute-start.33 = (bf16[1024,1024]{1,0:T(8,128)(2,1)}, bf16[1024,1024]{1,0:T(8,128)(2,1)S(1)}, u32[]{:S(2)}, u32[]{:S(2)}) collective-permute-start(bf16[1024,1024]{1,0:T(8,128)(2,1)} %shard_map.135.mine), channel_id=1, source_target_pairs={{0,1},{1,0},{2,3},{3,2},{4,5},{5,4},{6,7},{7,6},{8,9},{9,8},{10,11... | collective-permute-start | bytes 6291464 | tf_op jit(solution)/shard_map/ppermute | solution.py:494
  230.4 24.5 %collective-permute-start.43 = (bf16[4,4,16,640]{3,2,1,0:T(8,128)(2,1)}, bf16[4,4,16,640]{3,2,1,0:T(8,128)(2,1)S(1)}, u32[]{:S(2)}, u32[]{:S(2)}) collective-permute-start(bf16[4,4,16,640]{3,2,1,0:T(8,128)(2,1)} %bitcast.120), channel_id=1, source_target_pairs={{0,24},{1,25},{2,26},{3,27},{4,28},{5,29},{6,30},{7,31},{8,0},{9,1... | collective-permute-start | bytes 983048 | tf_op jit(solution)/shard_map/ppermute | solution.py:41
  232.7 25.5 %collective-permute-start.44 = (bf16[4,4,16,640]{3,2,1,0:T(8,128)(2,1)}, bf16[4,4,16,640]{3,2,1,0:T(8,128)(2,1)S(1)}, u32[]{:S(2)}, u32[]{:S(2)}) collective-permute-start(bf16[4,4,16,640]{3,2,1,0:T(8,128)(2,1)} %bitcast.118), channel_id=1, source_target_pairs={{0,16},{1,17},{2,18},{3,19},{4,20},{5,21},{6,22},{7,23},{8,24},{9,... | collective-permute-start | bytes 983048 | tf_op jit(solution)/shard_map/ppermute | solution.py:41
  232.7 44.1 %collective-permute-start.24 = (bf16[4,4,16,1280]{3,2,1,0:T(8,128)(2,1)}, bf16[4,4,16,1280]{3,2,1,0:T(8,128)(2,1)S(1)}, u32[]{:S(2)}, u32[]{:S(2)}) collective-permute-start(bf16[4,4,16,1280]{3,2,1,0:T(8,128)(2,1)} %bitcast.115), channel_id=1, source_target_pairs={{0,6},{1,97},{2,0},{3,99},{4,2},{5,101},{6,4},{7,103},{8,14},{9,10... | collective-permute-start | bytes 1966088 | tf_op jit(solution)/shard_map/ppermute | solution.py:41
  233.5 25.6 %collective-permute-start.45 = (bf16[4,4,16,640]{3,2,1,0:T(8,128)(2,1)}, bf16[4,4,16,640]{3,2,1,0:T(8,128)(2,1)S(1)}, u32[]{:S(2)}, u32[]{:S(2)}) collective-permute-start(bf16[4,4,16,640]{3,2,1,0:T(8,128)(2,1)} %bitcast.116), channel_id=1, source_target_pairs={{0,8},{1,9},{2,10},{3,11},{4,12},{5,13},{6,14},{7,15},{8,16},{9,17... | collective-permute-start | bytes 983048 | tf_op jit(solution)/shard_map/ppermute | solution.py:41
  254.9 16.9 %collective-permute-start.47 = (bf16[4,4,16,640]{3,2,1,0:T(8,128)(2,1)}, bf16[4,4,16,640]{3,2,1,0:T(8,128)(2,1)S(1)}, u32[]{:S(2)}, u32[]{:S(2)}) collective-permute-start(bf16[4,4,16,640]{3,2,1,0:T(8,128)(2,1)} %bitcast.119), channel_id=1, source_target_pairs={{0,16},{1,17},{2,18},{3,19},{4,20},{5,21},{6,22},{7,23},{8,24},{9,... | collective-permute-start | bytes 983048 | tf_op jit(solution)/shard_map/ppermute | solution.py:41
  259.1 25.2 %collective-permute-start.25 = (bf16[4,4,16,1280]{3,2,1,0:T(8,128)(2,1)}, bf16[4,4,16,1280]{3,2,1,0:T(8,128)(2,1)S(1)}, u32[]{:S(2)}, u32[]{:S(2)}) collective-permute-start(bf16[4,4,16,1280]{3,2,1,0:T(8,128)(2,1)} %bitcast.32), channel_id=1, source_target_pairs={{0,4},{1,65},{2,6},{3,67},{4,0},{5,69},{6,2},{7,71},{8,12},{9,73},... | collective-permute-start | bytes 1966088 | tf_op jit(solution)/shard_map/ppermute | solution.py:41
  265.3 21.5 %collective-permute-start.26 = (bf16[4,4,16,1280]{3,2,1,0:T(8,128)(2,1)}, bf16[4,4,16,1280]{3,2,1,0:T(8,128)(2,1)S(1)}, u32[]{:S(2)}, u32[]{:S(2)}) collective-permute-start(bf16[4,4,16,1280]{3,2,1,0:T(8,128)(2,1)} %bitcast.33), channel_id=1, source_target_pairs={{0,2},{1,33},{2,4},{3,35},{4,6},{5,37},{6,0},{7,39},{8,10},{9,41},... | collective-permute-start | bytes 1966088 | tf_op jit(solution)/shard_map/ppermute | solution.py:41
  273.3 19.3 %collective-permute-start.35 = (bf16[4,4,16,1280]{3,2,1,0:T(8,128)(2,1)}, bf16[4,4,16,1280]{3,2,1,0:T(8,128)(2,1)S(1)}, u32[]{:S(2)}, u32[]{:S(2)}) collective-permute-start(bf16[4,4,16,1280]{3,2,1,0:T(8,128)(2,1)} %bitcast.113), channel_id=1, source_target_pairs={{0,4},{1,65},{2,6},{3,67},{4,0},{5,69},{6,2},{7,71},{8,12},{9,73},... | collective-permute-start | bytes 1966088 | tf_op jit(solution)/shard_map/ppermute | solution.py:41
  276.9 16.8 %collective-permute-start.36 = (bf16[4,4,16,1280]{3,2,1,0:T(8,128)(2,1)}, bf16[4,4,16,1280]{3,2,1,0:T(8,128)(2,1)}, u32[]{:S(2)}, u32[]{:S(2)}) collective-permute-start(bf16[4,4,16,1280]{3,2,1,0:T(8,128)(2,1)} %bitcast.112), channel_id=1, source_target_pairs={{0,2},{1,33},{2,4},{3,35},{4,6},{5,37},{6,0},{7,39},{8,10},{9,41},... | collective-permute-start | bytes 1966088 | tf_op jit(solution)/shard_map/ppermute | solution.py:41
  284.3 27.9 %collective-permute-start.49 = (bf16[4,128,640]{2,1,0:T(8,128)(2,1)}, bf16[4,128,640]{2,1,0:T(8,128)(2,1)}, u32[]{:S(2)}, u32[]{:S(2)}) collective-permute-start(bf16[4,128,640]{2,1,0:T(8,128)(2,1)} %get-tuple-element.98), channel_id=1, source_target_pairs={{0,96},{1,97},{2,98},{3,99},{4,100},{5,101},{6,102},{7,103},{8,104... | collective-permute-start | bytes 1966088 | tf_op jit(solution)/shard_map/ppermute | solution.py:41
  301.7 37.7 %collective-permute-start.37 = (bf16[4,128,1280]{2,1,0:T(8,128)(2,1)}, bf16[4,128,1280]{2,1,0:T(8,128)(2,1)S(1)}, u32[]{:S(2)}, u32[]{:S(2)}) collective-permute-start(bf16[4,128,1280]{2,1,0:T(8,128)(2,1)} %get-tuple-element.86), channel_id=1, source_target_pairs={{0,24},{1,7},{2,26},{3,1},{4,28},{5,3},{6,30},{7,5},{8,0},{9,15},{... | collective-permute-start | bytes 3932168 | tf_op jit(solution)/shard_map/ppermute | solution.py:41
  305.1 34.3 %collective-permute-start.38 = (bf16[4,128,1280]{2,1,0:T(8,128)(2,1)}, bf16[4,128,1280]{2,1,0:T(8,128)(2,1)S(1)}, u32[]{:S(2)}, u32[]{:S(2)}) collective-permute-start(bf16[4,128,1280]{2,1,0:T(8,128)(2,1)} %get-tuple-element.87), channel_id=1, source_target_pairs={{0,16},{1,5},{2,18},{3,7},{4,20},{5,1},{6,22},{7,3},{8,24},{9,13},... | collective-permute-start | bytes 3932168 | tf_op jit(solution)/shard_map/ppermute | solution.py:41
  307.6 31.8 %collective-permute-start.39 = (bf16[4,128,1280]{2,1,0:T(8,128)(2,1)}, bf16[4,128,1280]{2,1,0:T(8,128)(2,1)S(1)}, u32[]{:S(2)}, u32[]{:S(2)}) collective-permute-start(bf16[4,128,1280]{2,1,0:T(8,128)(2,1)} %get-tuple-element.88), channel_id=1, source_target_pairs={{0,8},{1,3},{2,10},{3,5},{4,12},{5,7},{6,14},{7,1},{8,16},{9,11},{... | collective-permute-start | bytes 3932168 | tf_op jit(solution)/shard_map/ppermute | solution.py:41
  310.2 19.3 %collective-permute-start.50 = (bf16[4,128,640]{2,1,0:T(8,128)(2,1)}, bf16[4,128,640]{2,1,0:T(8,128)(2,1)S(1)}, u32[]{:S(2)}, u32[]{:S(2)}) collective-permute-start(bf16[4,128,640]{2,1,0:T(8,128)(2,1)} %get-tuple-element.99), channel_id=1, source_target_pairs={{0,64},{1,65},{2,66},{3,67},{4,68},{5,69},{6,70},{7,71},{8,72},{9,... | collective-permute-start | bytes 1966088 | tf_op jit(solution)/shard_map/ppermute | solution.py:41
  312.3 24.7 %collective-permute-start.51 = (bf16[4,128,640]{2,1,0:T(8,128)(2,1)}, bf16[4,128,640]{2,1,0:T(8,128)(2,1)S(1)}, u32[]{:S(2)}, u32[]{:S(2)}) collective-permute-start(bf16[4,128,640]{2,1,0:T(8,128)(2,1)} %get-tuple-element.100), channel_id=1, source_target_pairs={{0,32},{1,33},{2,34},{3,35},{4,36},{5,37},{6,38},{7,39},{8,40},{9,... | collective-permute-start | bytes 1966088 | tf_op jit(solution)/shard_map/ppermute | solution.py:41
  340.8 15.9 %collective-permute-start.42 = (bf16[128,1280]{1,0:T(8,128)(2,1)S(1)}, bf16[128,1280]{1,0:T(8,128)(2,1)S(1)}, u32[]{:S(2)}, u32[]{:S(2)}) collective-permute-start(bf16[128,1280]{1,0:T(8,128)(2,1)S(1)} %get-tuple-element.105), channel_id=1, source_target_pairs={{0,32},{1,9},{2,34},{3,11},{4,36},{5,13},{6,38},{7,15},{8,40},{9,1... | collective-permute-start | bytes 983048 | tf_op jit(solution)/shard_map/ppermute | solution.py:41
  341.0 15.7 %collective-permute-start.41 = (bf16[128,1280]{1,0:T(8,128)(2,1)S(1)}, bf16[128,1280]{1,0:T(8,128)(2,1)S(1)}, u32[]{:S(2)}, u32[]{:S(2)}) collective-permute-start(bf16[128,1280]{1,0:T(8,128)(2,1)S(1)} %get-tuple-element.106), channel_id=1, source_target_pairs={{0,64},{1,17},{2,66},{3,19},{4,68},{5,21},{6,70},{7,23},{8,72},{9,... | collective-permute-start | bytes 983048 | tf_op jit(solution)/shard_map/ppermute | solution.py:41
  (63 other events, 736.2 us)
